TPU v7x, 8 devices: a whole 2x2x1 slice. The times are simulated.
8 devices in a mesh: dp: 1 (over z), yz: 2 (over y), x: 4 (over x, core).
Axes of the slice: x: 2, y: 2, z: 1, core: 2. Of those that a mesh axis runs over, the one named last changes fastest.
Arguments:
- hidden: bfloat16 [64, 4096], P('dp', ('x', 'yz'))
- norm_gain: bfloat16 [3, 4096], P(None, 'x')
- w_q: bfloat16 [3, 4096, 4096], P(None, 'x', 'yz')
- w_kv: bfloat16 [3, 4096, 512], P(None, 'x', 'yz')
- w_gate: bfloat16 [3, 4096, 16384], P(None, 'x', 'yz')
- w_up: bfloat16 [3, 4096, 16384], P(None, 'x', 'yz')
- w_o: bfloat16 [3, 4096, 4096], P(None, 'yz', 'x')
- w_down: bfloat16 [3, 16384, 4096], P(None, 'yz', 'x')
- k_cache: bfloat16 [3, 64, 256, 256], P(None, ('dp', 'x', 'yz'))
- v_cache: bfloat16 [3, 64, 256, 256], P(None, ('dp', 'x', 'yz'))
- seq_len: int32 [64], P(('dp', 'x', 'yz'))
Outputs:
- output 1: bfloat16 [64, 4096], P('dp', ('x', 'yz'))
- output 2: bfloat16 [3, 64, 256, 256], P(None, ('dp', 'x', 'yz'))
- output 3: bfloat16 [3, 64, 256, 256], P(None, ('dp', 'x', 'yz'))
All inputs are finite; a program needn't handle non-finite values.
Results may differ from a plain program's by a relative error of at most 0.02.
Values are sent between devices in bfloat16 or wider.
A program may use at most 1 GiB of HBM per device.

v0:
```python
import jax
import jax.numpy as jnp
from jax import lax
from jax.sharding import PartitionSpec as P

NORM_EPS = 1e-6


def solution(mesh):
    x_size = mesh.shape["x"]
    y_size = mesh.shape["yz"]
    row_spec = P("dp", ("x", "yz"))
    tile_in = P(None, "x", "yz")
    tile_out = P(None, "yz", "x")
    cache_spec = P(None, ("dp", "x", "yz"))
    len_spec = P(("dp", "x", "yz"))

    def device_step(hidden, norm_gain, w_q, w_kv, w_gate, w_up, w_o, w_down, k_cache, v_cache, seq_len):
        d_model = hidden.shape[1] * x_size * y_size
        local_seqs = k_cache.shape[1]
        cache_len = k_cache.shape[2]
        head_dim = k_cache.shape[3]
        q_cols = w_q.shape[2]
        kv_cols = w_kv.shape[2]
        ff_cols = w_gate.shape[2]
        attn_cols = q_cols + kv_cols
        n_heads = q_cols * y_size // head_dim
        positions = jnp.arange(cache_len)
        slot_hit = (positions[None, :] == seq_len[:, None])[:, :, None]
        visible = positions[None, None, :] <= seq_len[:, None, None]
        k_layers = []
        v_layers = []
        for layer_idx in range(w_q.shape[0]):
            feat_rows = lax.all_gather(hidden, "yz", axis=1, tiled=True)
            feat_f32 = feat_rows.astype(jnp.float32)
            sq_sum = lax.psum(jnp.sum(feat_f32 * feat_f32, axis=1, keepdims=True), "x")
            inv_rms = lax.rsqrt(sq_sum / d_model + NORM_EPS)
            normed = (feat_f32 * inv_rms * norm_gain[layer_idx].astype(jnp.float32)).astype(jnp.bfloat16)
            part_sum = jnp.concatenate([jnp.dot(normed, weight[layer_idx], preferred_element_type=jnp.float32) for weight in (w_q, w_kv, w_gate, w_up)], axis=1).astype(jnp.bfloat16)
            proj_rows = lax.psum_scatter(part_sum, "x", scatter_dimension=0, tiled=True)
            gate_act = proj_rows[:, attn_cols:attn_cols + ff_cols].astype(jnp.float32)
            up_act = proj_rows[:, attn_cols + ff_cols:].astype(jnp.float32)
            mlp_act = (jax.nn.silu(gate_act) * up_act).astype(jnp.bfloat16)
            mlp_rows = lax.all_gather(mlp_act, "x", axis=0, tiled=True)
            by_seq = lax.all_to_all(proj_rows[:, :attn_cols], "yz", 0, 1, tiled=True).reshape(local_seqs, y_size, attn_cols)
            query_heads = by_seq[:, :, :q_cols].reshape(local_seqs, n_heads, head_dim)
            kv_new = by_seq[:, :, q_cols:].reshape(local_seqs, 2 * head_dim)
            new_k = jnp.where(slot_hit, kv_new[:, None, :head_dim], k_cache[layer_idx])
            new_v = jnp.where(slot_hit, kv_new[:, None, head_dim:], v_cache[layer_idx])
            scores = jnp.einsum("bhd,bsd->bhs", query_heads, new_k, preferred_element_type=jnp.float32) * head_dim ** -0.5
            scores = jnp.where(visible, scores, -1e30)
            weights = jnp.exp(scores - jnp.max(scores, axis=-1, keepdims=True))
            probs_bf = (weights / jnp.sum(weights, axis=-1, keepdims=True)).astype(jnp.bfloat16)
            attn_out = jnp.einsum("bhs,bsd->bhd", probs_bf, new_v, preferred_element_type=jnp.float32).astype(jnp.bfloat16)
            attn_back = lax.all_to_all(attn_out.reshape(local_seqs, n_heads * head_dim), "yz", 1, 0, tiled=True)
            attn_rows = lax.all_gather(attn_back, "x", axis=0, tiled=True)
            update = jnp.dot(attn_rows, w_o[layer_idx], preferred_element_type=jnp.float32) + jnp.dot(mlp_rows, w_down[layer_idx], preferred_element_type=jnp.float32)
            update = lax.psum_scatter(update.astype(jnp.bfloat16), "yz", scatter_dimension=1, tiled=True)
            hidden = (hidden.astype(jnp.float32) + update.astype(jnp.float32)).astype(jnp.bfloat16)
            k_layers.append(new_k)
            v_layers.append(new_v)
        return hidden, jnp.stack(k_layers), jnp.stack(v_layers)

    sharded_step = jax.shard_map(
        device_step,
        mesh=mesh,
        in_specs=(row_spec, P(None, "x"), tile_in, tile_in, tile_in, tile_in, tile_out, tile_out, cache_spec, cache_spec, len_spec),
        out_specs=(row_spec, cache_spec, cache_spec),
        check_vma=False,
    )
    return sharded_step
```

profile of v0, /device:TPU:0, one launch (start us, length us, event | category | flops | bytes accessed | tf_op | source)
XLA Modules:
  0.0 346.0 jit_solution(5160343421088703773)
XLA Ops:
  8.0 6.3 %all_gather.27 = bf16[64,1024]{1,0:T(8,128)(2,1)S(1)} all-gather(bf16[64,512]{1,0:T(8,128)(2,1)} %param.11), channel_id=1, replica_groups=mesh['dp'=1,'yz'=2,'x'=4] {'yz'}, dimensions={1}, use_global_device_ids=true | all-gather | bytes 196608 | tf_op jit(solution)/shard_map/all_gather | solution.py:34
  14.4 5.9 %psum.21 = f32[64,1]{0,1:T(1,128)S(1)} all-reduce(f32[64,1]{0,1:T(1,128)S(1)} %bitcast.174), channel_id=1, replica_groups=mesh['dp'=1,'yz'=2,'x'=4] {'x'}, use_global_device_ids=true, to_apply=%region_1.0 | all-reduce | flops 64 | bytes 512 | tf_op jit(solution)/shard_map/psum | solution.py:36
  24.8 7.5 %fusion.30 = bf16[64,8192]{1,0:T(8,128)(2,1)S(1)} fusion(bf16[3,1024,8192]{2,1,0:T(8,128)(2,1)} %param.15, bf16[64,1024]{1,0:T(8,128)(2,1)S(1)} %all_gather.27, f32[1024]{0:T(1024)S(1)} %bitcast.172, f32[64]{0:T(128)S(1)} %rsqrt_bitcast_fusion.2), kind=kOutput, calls=%fused_computation.30 | convolution fusion | flops 1074528256 | bytes 17961216 | tf_op jit(solution)/shard_map/dot_general | solution.py:39
  32.3 7.5 %fusion.33 = bf16[64,8192]{1,0:T(8,128)(2,1)S(1)} fusion(bf16[3,1024,8192]{2,1,0:T(8,128)(2,1)} %param.16, bf16[64,1024]{1,0:T(8,128)(2,1)S(1)} %all_gather.27, f32[1024]{0:T(1024)S(1)} %bitcast.173, f32[64]{0:T(128)S(1)} %rsqrt_bitcast_fusion.2), kind=kOutput, calls=%fused_computation.31 | convolution fusion | flops 1074528256 | bytes 17961216 | tf_op jit(solution)/shard_map/dot_general | solution.py:39
  41.5 28.9 %reduce-scatter.7.cloned.1.call-done = bf16[16,18688]{1,0:T(8,128)(2,1)} async-done(((bf16[64,18688]{1,0:T(8,128)(2,1)}), bf16[16,18688]{1,0:T(8,128)(2,1)}) %reduce-scatter.7.cloned.1.call-update) | async-done | bytes 598032 | tf_op jit(solution)/shard_map/reduce_scatter | solution.py:40
  83.9 6.5 %all_to_all.105 = bf16[8,2,2048]{2,0,1:T(8,128)(2,1)S(1)} all-to-all(bf16[8,2,2048]{2,0,1:T(8,128)(2,1)S(1)} %copy.18), channel_id=1, replica_groups=mesh['dp'=1,'yz'=2,'x'=4] {'yz'}, dimensions={1} | all-to-all | bytes 131072 | tf_op jit(solution)/shard_map/all_to_all | solution.py:55
  90.4 7.8 %all_gather.28 = bf16[64,2048]{1,0:T(8,128)(2,1)S(1)} all-gather(bf16[16,2048]{1,0:T(8,128)(2,1)S(1)} %bitcast.157), channel_id=1, replica_groups=mesh['dp'=1,'yz'=2,'x'=4] {'x'}, dimensions={0}, use_global_device_ids=true | all-gather | bytes 327680 | tf_op jit(solution)/shard_map/all_gather | solution.py:56
  101.3 9.8 %fusion.93 = bf16[64,1024]{1,0:T(8,128)(2,1)} fusion(f32[64,1024]{1,0:T(8,128)S(1)} %fusion.56, bf16[64,8192]{1,0:T(8,128)(2,1)} %all-gather.4.cloned.1.call-done, bf16[3,8192,1024]{2,1,0:T(8,128)(2,1)} %param.18), kind=kOutput, calls=%fused_computation.70 | convolution fusion | flops 1073872896 | bytes 18219008 | tf_op jit(solution)/shard_map/dot_general | solution.py:57
  111.1 7.9 %reduce-scatter.9.cloned.1.call-done = bf16[64,512]{1,0:T(8,128)(2,1)} async-done(((bf16[64,1024]{1,0:T(8,128)(2,1)}), bf16[64,512]{1,0:T(8,128)(2,1)}) %reduce-scatter.9.cloned.1.call-update) | async-done | bytes 65552 | tf_op jit(solution)/shard_map/reduce_scatter | solution.py:58
  124.9 5.8 %psum.22 = f32[64,1]{0,1:T(1,128)S(1)} all-reduce(f32[64,1]{0,1:T(1,128)S(1)} %bitcast.175), channel_id=1, replica_groups=mesh['dp'=1,'yz'=2,'x'=4] {'x'}, use_global_device_ids=true, to_apply=%region_7.8 | all-reduce | flops 64 | bytes 512 | tf_op jit(solution)/shard_map/psum | solution.py:36
  135.2 7.5 %fusion.36 = bf16[64,8192]{1,0:T(8,128)(2,1)S(1)} fusion(bf16[3,1024,8192]{2,1,0:T(8,128)(2,1)} %param.15, bf16[64,1024]{1,0:T(8,128)(2,1)S(1)} %all_gather.30, f32[1024]{0:T(1024)S(1)} %bitcast.168, f32[64]{0:T(128)S(1)} %rsqrt_bitcast_fusion.1), kind=kOutput, calls=%fused_computation.32 | convolution fusion | flops 1074528256 | bytes 17961216 | tf_op jit(solution)/shard_map/dot_general | solution.py:39
  142.7 7.5 %fusion.39 = bf16[64,8192]{1,0:T(8,128)(2,1)S(1)} fusion(bf16[3,1024,8192]{2,1,0:T(8,128)(2,1)} %param.16, bf16[64,1024]{1,0:T(8,128)(2,1)S(1)} %all_gather.30, f32[1024]{0:T(1024)S(1)} %bitcast.169, f32[64]{0:T(128)S(1)} %rsqrt_bitcast_fusion.1), kind=kOutput, calls=%fused_computation.33 | convolution fusion | flops 1074528256 | bytes 17961216 | tf_op jit(solution)/shard_map/dot_general | solution.py:39
  151.9 27.7 %reduce-scatter.11.cloned.1.call-done = bf16[16,18688]{1,0:T(8,128)(2,1)} async-done(((bf16[64,18688]{1,0:T(8,128)(2,1)}), bf16[16,18688]{1,0:T(8,128)(2,1)}) %reduce-scatter.11.cloned.1.call-update) | async-done | bytes 598032 | tf_op jit(solution)/shard_map/reduce_scatter | solution.py:40
  182.4 6.7 %all_to_all.106 = bf16[2,8,2304]{2,1,0:T(8,128)(2,1)S(1)} all-to-all(bf16[2,8,2304]{2,1,0:T(8,128)(2,1)S(1)} %slice_bitcast_fusion.1), channel_id=1, replica_groups=mesh['dp'=1,'yz'=2,'x'=4] {'yz'}, dimensions={0} | all-to-all | bytes 147456 | tf_op jit(solution)/shard_map/all_to_all | solution.py:45
  191.9 6.5 %all_to_all.107 = bf16[8,2,2048]{2,0,1:T(8,128)(2,1)S(1)} all-to-all(bf16[8,2,2048]{2,0,1:T(8,128)(2,1)S(1)} %copy.20), channel_id=1, replica_groups=mesh['dp'=1,'yz'=2,'x'=4] {'yz'}, dimensions={1} | all-to-all | bytes 131072 | tf_op jit(solution)/shard_map/all_to_all | solution.py:55
  198.4 8.0 %all_gather.31 = bf16[64,2048]{1,0:T(8,128)(2,1)S(1)} all-gather(bf16[16,2048]{1,0:T(8,128)(2,1)S(1)} %bitcast.158), channel_id=1, replica_groups=mesh['dp'=1,'yz'=2,'x'=4] {'x'}, dimensions={0}, use_global_device_ids=true | all-gather | bytes 327680 | tf_op jit(solution)/shard_map/all_gather | solution.py:56
  210.2 9.7 %fusion.90 = bf16[64,1024]{1,0:T(8,128)(2,1)} fusion(f32[64,1024]{1,0:T(8,128)} %fusion.52, bf16[64,8192]{1,0:T(8,128)(2,1)} %all-gather.6.cloned.1.call-done, bf16[3,8192,1024]{2,1,0:T(8,128)(2,1)} %param.18), kind=kOutput, calls=%fused_computation.69 | convolution fusion | flops 1073872896 | bytes 18219008 | tf_op jit(solution)/shard_map/dot_general | solution.py:57
  219.9 7.6 %reduce-scatter.13.cloned.1.call-done = bf16[64,512]{1,0:T(8,128)(2,1)} async-done(((bf16[64,1024]{1,0:T(8,128)(2,1)}), bf16[64,512]{1,0:T(8,128)(2,1)}) %reduce-scatter.13.cloned.1.call-update) | async-done | bytes 65552 | tf_op jit(solution)/shard_map/reduce_scatter | solution.py:58
  233.5 5.9 %psum.23 = f32[64,1]{0,1:T(1,128)S(1)} all-reduce(f32[64,1]{0,1:T(1,128)S(1)} %bitcast.176), channel_id=1, replica_groups=mesh['dp'=1,'yz'=2,'x'=4] {'x'}, use_global_device_ids=true, to_apply=%region_13.14 | all-reduce | flops 64 | bytes 512 | tf_op jit(solution)/shard_map/psum | solution.py:36
  243.8 7.5 %fusion.42 = bf16[64,8192]{1,0:T(8,128)(2,1)S(1)} fusion(bf16[3,1024,8192]{2,1,0:T(8,128)(2,1)} %param.15, bf16[64,1024]{1,0:T(8,128)(2,1)S(1)} %all_gather.33, f32[1024]{0:T(1024)S(1)} %bitcast.164, f32[64]{0:T(128)S(1)} %rsqrt_bitcast_fusion), kind=kOutput, calls=%fused_computation.34 | convolution fusion | flops 1074528256 | bytes 17961216 | tf_op jit(solution)/shard_map/dot_general | solution.py:39
  251.3 7.5 %fusion.45 = bf16[64,8192]{1,0:T(8,128)(2,1)S(1)} fusion(bf16[3,1024,8192]{2,1,0:T(8,128)(2,1)} %param.16, bf16[64,1024]{1,0:T(8,128)(2,1)S(1)} %all_gather.33, f32[1024]{0:T(1024)S(1)} %bitcast.165, f32[64]{0:T(128)S(1)} %rsqrt_bitcast_fusion), kind=kOutput, calls=%fused_computation.35 | convolution fusion | flops 1074528256 | bytes 17961216 | tf_op jit(solution)/shard_map/dot_general | solution.py:39
  260.4 27.8 %reduce-scatter.15.cloned.1.call-done = bf16[16,18688]{1,0:T(8,128)(2,1)} async-done(((bf16[64,18688]{1,0:T(8,128)(2,1)}), bf16[16,18688]{1,0:T(8,128)(2,1)}) %reduce-scatter.15.cloned.1.call-update) | async-done | bytes 598032 | tf_op jit(solution)/shard_map/reduce_scatter | solution.py:40
  308.0 7.8 %all_gather.34 = bf16[64,2048]{1,0:T(8,128)(2,1)S(1)} all-gather(bf16[16,2048]{1,0:T(8,128)(2,1)S(1)} %bitcast.156), channel_id=1, replica_groups=mesh['dp'=1,'yz'=2,'x'=4] {'x'}, dimensions={0}, use_global_device_ids=true | all-gather | bytes 327680 | tf_op jit(solution)/shard_map/all_gather | solution.py:56
  318.9 9.8 %fusion.87 = bf16[64,1024]{1,0:T(8,128)(2,1)} fusion(f32[64,1024]{1,0:T(8,128)S(1)} %fusion.48, bf16[64,8192]{1,0:T(8,128)(2,1)} %all-gather.8.cloned.1.call-done, bf16[3,8192,1024]{2,1,0:T(8,128)(2,1)} %param.18), kind=kOutput, calls=%fused_computation.68 | convolution fusion | flops 1073872896 | bytes 18219008 | tf_op jit(solution)/shard_map/dot_general | solution.py:57
  (97 shorter events, 90.3 us)
Async XLA Ops:
  7.2 63.3 %reduce-scatter.7.cloned.1.call-start = ((), (), s32[]{:S(2)}) async-start(), calls=%async_computation.12 | async-start | bytes 2990080 | tf_op jit(solution)/shard_map/reduce_scatter | solution.py:40
  39.8 37.4 %copy-start.2 = (s32[8]{0:T(128)S(1)}, s32[8]{0:T(128)}, u32[]{:S(2)}) copy-start(s32[8]{0:T(128)} %param.21) | copy-start | bytes 100
  39.8 43.3 %copy-start = (bf16[3,8,256,256]{3,2,1,0:T(8,128)(2,1)S(1)}, bf16[3,8,256,256]{3,2,1,0:T(8,128)(2,1)}, u32[]{:S(2)}) copy-start(bf16[3,8,256,256]{3,2,1,0:T(8,128)(2,1)} %param.20) | copy-start | bytes 9437188
  41.4 59.8 %all-gather.4.cloned.1.call-start = ((), (), s32[]{:S(2)}) async-start(), calls=%async_computation.13 | async-start | bytes 1310720 | tf_op jit(solution)/shard_map/all_gather | solution.py:44
  73.9 7.3 %all-to-all-start = ((bf16[2,8,2304]{2,1,0:T(8,128)(2,1)}), bf16[2,8,2304]{2,1,0:T(8,128)(2,1)S(1)}, u32[]{:S(2)}, u32[]{:S(2)}) async-start(bf16[2,8,2304]{2,1,0:T(8,128)(2,1)} %slice_bitcast_fusion.2), calls=%async_computation.1 | async-start | bytes 147456 | tf_op jit(solution)/shard_map/all_to_all | solution.py:45
  77.2 41.8 %reduce-scatter.9.cloned.1.call-start = ((), (), s32[]{:S(2)}) async-start(), calls=%async_computation.14 | async-start | bytes 196608 | tf_op jit(solution)/shard_map/reduce_scatter | solution.py:58
  101.2 17.8 %copy-start.1 = (bf16[64,512]{1,0:T(8,128)(2,1)S(1)}, bf16[64,512]{1,0:T(8,128)(2,1)}, u32[]{:S(2)}) copy-start(bf16[64,512]{1,0:T(8,128)(2,1)} %param.11) | copy-start | bytes 196612
  111.1 68.5 %reduce-scatter.11.cloned.1.call-start = ((), (), s32[]{:S(2)}) async-start(), calls=%async_computation.15 | async-start | bytes 2990080 | tf_op jit(solution)/shard_map/reduce_scatter | solution.py:40
  151.8 58.3 %all-gather.6.cloned.1.call-start = ((), (), s32[]{:S(2)}) async-start(), calls=%async_computation.16 | async-start | bytes 1310720 | tf_op jit(solution)/shard_map/all_gather | solution.py:44
  181.5 46.1 %reduce-scatter.13.cloned.1.call-start = ((), (), s32[]{:S(2)}) async-start(), calls=%async_computation.17 | async-start | bytes 196608 | tf_op jit(solution)/shard_map/reduce_scatter | solution.py:58
  219.9 68.3 %reduce-scatter.15.cloned.1.call-start = ((), (), s32[]{:S(2)}) async-start(), calls=%async_computation.18 | async-start | bytes 2990080 | tf_op jit(solution)/shard_map/reduce_scatter | solution.py:40
  289.7 7.3 %all-to-all-start.4 = ((bf16[2,8,2304]{2,1,0:T(8,128)(2,1)}), bf16[2,8,2304]{2,1,0:T(8,128)(2,1)S(1)}, u32[]{:S(2)}, u32[]{:S(2)}) async-start(bf16[2,8,2304]{2,1,0:T(8,128)(2,1)} %slice_bitcast_fusion), calls=%async_computation.9 | async-start | bytes 147456 | tf_op jit(solution)/shard_map/all_to_all | solution.py:45
  293.0 25.9 %all-gather.8.cloned.1.call-start = ((), (), s32[]{:S(2)}) async-start(), calls=%async_computation.19 | async-start | bytes 1310720 | tf_op jit(solution)/shard_map/all_gather | solution.py:44
  300.4 7.7 %all-to-all-start.5 = ((bf16[8,2,2048]{2,0,1:T(8,128)(2,1)}), bf16[8,2,2048]{2,0,1:T(8,128)(2,1)S(1)}, u32[]{:S(2)}, u32[]{:S(2)}) async-start(bf16[8,2,2048]{2,0,1:T(8,128)(2,1)} %copy.22), calls=%async_computation.10 | async-start | bytes 131072 | tf_op jit(solution)/shard_map/all_to_all | solution.py:55
  303.7 34.3 %reduce-scatter.17.cloned.1.call-start = ((), (), s32[]{:S(2)}) async-start(), calls=%async_computation.20 | async-start | bytes 196608 | tf_op jit(solution)/shard_map/reduce_scatter | solution.py:58
Sparse Core Ops, SparseCore 0:
  41.6 28.8 reduce-scatter.6
  72.5 13.6 all-gather.3
  111.2 7.7 reduce-scatter.8
  151.9 27.5 reduce-scatter.10
  181.6 13.7 all-gather.5
  220.0 7.5 reduce-scatter.12
  260.5 27.6 reduce-scatter.14
  295.9 14.2 all-gather.7
  328.8 9.1 reduce-scatter.16
where the time goes:
time: 348 us; the launch traced here: 346 us
  waiting for transfers between devices  111 us (32%)
  matrix products  104 us (30%)
  blocking collectives  77.1 us (22%)
  other arithmetic  24.1 us (7%)
  between operations  14.2 us (4%)
  starting transfers between devices  10.3 us (3%)
  local copies, waits for them, and re-layouts  5.12 us (1%)
    reduce_scatter x3, waiting for transfers between devices, device_step(): proj_rows = lax.psum_scatter(part_sum, 'x', scatter_dimension=0, tiled=True)  84.4 us
    dot_general x12, matrix products, device_step(): jnp.dot(normed, weight[layer_idx], preferred_element_type=jnp.float32)  58.2 us
    dot_general x3, matrix products, device_step(): jnp.dot(mlp_rows, w_down[layer_idx], preferred_element_type=jnp.float32)  29.3 us
    all_gather x3, blocking collectives, device_step(): attn_rows = lax.all_gather(attn_back, 'x', axis=0, tiled=True)  23.7 us
    reduce_scatter x3, waiting for transfers between devices, device_step(): lax.psum_scatter(update.astype(jnp.bfloat16), 'yz', scatter_dimension=1,...  20.4 us
    psum x3, blocking collectives, device_step(): sq_sum = lax.psum(jnp.sum(feat_f32 * feat_f32, axis=1, keepdims=True), 'x')  17.7 us
    all_gather x3, blocking collectives, device_step(): feat_rows = lax.all_gather(hidden, 'yz', axis=1, tiled=True)  16.1 us
    all_to_all x2, blocking collectives, device_step(): lax.all_to_all(attn_out.reshape(local_seqs, n_heads * head_dim), 'yz', 1,...  13 us
  transfers between devices with their start and end apart: 12, of which 8 were waited for; matrix products, arithmetic and copies ran while one was open for 9% of the time, Pallas kernels for 0%

commit v1 on v0

v1 whole, which is shorter than its diff:
```python
import functools

import jax
import jax.numpy as jnp
from jax import lax
from jax.experimental import pallas as pl
from jax.experimental.pallas import tpu as pltpu
from jax.sharding import PartitionSpec as P

NORM_EPS = 1e-6
MESH = pl.DeviceIdType.MESH
BF = jnp.bfloat16
F32 = jnp.float32

NG = 7
ND = 7
LAG_B, LAG_C, LAG_D, LAG_E = 1, 3, 5, 6


def step_kernel(dims, hid, gain, wq, wkv, wg, wu, wo, wd, kc, vc, lens,
                hout, knew, vnew,
                wq_b, wkv_b, wg_b, wu_b, wo_b, wd_b, k_b, v_b,
                hin, h_b, u_b, acc, ss_s, ss_r,
                part, rb, ib, m_all, part_q, rb_q, ib_q, zq, yq, ob, o_all, yx_s, yx_r,
                sem_wq, sem_wkv, sem_g, sem_u, sem_wo, sem_d, sem_k, sem_v,
                sem_h, sem_ss, sem_rb, sem_ib, sem_mp, sem_mq, sem_mf,
                sem_zq, sem_oy, sem_op, sem_oq, sem_of, sem_yx):
    L, CH, NCH, D = dims["layers"], dims["chunk"], dims["n_chunks"], dims["d"]
    HD = 256
    QC = wq_b.shape[1]
    x = lax.axis_index("x")
    y = lax.axis_index("yz")
    c = lax.rem(x, 2)
    cx = x // 2
    xp = x + 1 - 2 * c
    xq = lax.rem(x + 2, 4)
    xd = 3 - x
    dev_p, dev_q, dev_d, dev_y = {"x": xp}, {"x": xq}, {"x": xd}, {"yz": 1 - y}

    def rc(src, dst, sems, dev):
        return pltpu.make_async_remote_copy(
            src_ref=src, dst_ref=dst, send_sem=sems[0], recv_sem=sems[1],
            device_id=dev, device_id_type=MESH)

    def sp(s, *idx):
        return (s.at[(0,) + idx], s.at[(1,) + idx])

    def cp_q(l):
        return (pltpu.make_async_copy(wq.at[l], wq_b, sem_wq),
                pltpu.make_async_copy(wkv.at[l], wkv_b, sem_wkv))

    def cp_gu(i):
        l, j, s = i // NCH, lax.rem(i, NCH), lax.rem(i, NG)
        cols = pl.ds(pl.multiple_of(j * CH, CH), CH)
        return (pltpu.make_async_copy(wg.at[l, :, cols], wg_b.at[s], sem_g.at[s]),
                pltpu.make_async_copy(wu.at[l, :, cols], wu_b.at[s], sem_u.at[s]))

    def cp_d(i):
        l, j, s = i // NCH, lax.rem(i, NCH), lax.rem(i, ND)
        rows = pl.ds(pl.multiple_of(j * CH, CH), CH)
        return (pltpu.make_async_copy(wd.at[l, rows, :], wd_b.at[s], sem_d.at[s]),)

    def cp_o(l):
        return (pltpu.make_async_copy(wo.at[l], wo_b, sem_wo),)

    def cp_kv(l):
        return (pltpu.make_async_copy(kc.at[l], k_b, sem_k),
                pltpu.make_async_copy(vc.at[l], v_b, sem_v))

    def start(cs):
        for cpy in cs:
            cpy.start()

    def wait(cs):
        for cpy in cs:
            cpy.wait()

    start(cp_q(0))
    start(cp_gu(0))

    barrier = pltpu.get_barrier_semaphore()
    for dev in (dev_p, dev_q, dev_d, dev_y):
        pl.semaphore_signal(barrier, inc=1, device_id=dev, device_id_type=MESH)
    pl.semaphore_wait(barrier, 4)

    h_send = rc(hid, hin.at[y], sp(sem_h), dev_y)
    h_send.start()
    hin[y] = hid[...]
    start(cp_gu(1))
    rc(hid, hin.at[1 - y], sp(sem_h), dev_y).wait_recv()
    half = hid.shape[1]
    h_b[:, :half] = hin[0]
    h_b[:, half:] = hin[1]
    h_send.wait_send()

    rows = h_b.shape[0]
    eye = (lax.broadcasted_iota(jnp.int32, (rows, 128), 0)
           == lax.broadcasted_iota(jnp.int32, (rows, 128), 1))

    def norm(l):
        h = h_b[...].astype(F32)
        ss = jnp.sum(h * h, axis=1, keepdims=True)
        ss_row = jnp.sum(jnp.where(eye, ss, 0.0), axis=0, keepdims=True)
        ss_s[...] = jnp.broadcast_to(ss_row, ss_s.shape)
        cps = [rc(ss_s, ss_r.at[k], sp(sem_ss, k), dev)
               for k, dev in enumerate((dev_p, dev_q, dev_d))]
        for cpy in cps:
            cpy.start()
        gall = gain[...].astype(F32)
        g = gall[0:1]
        for k in range(1, L):
            g = jnp.where(l == k, gall[k:k + 1], g)
        for cpy in cps:
            cpy.wait()
        tot = (ss_s[0:1] + ss_r[0, 0:1]) + (ss_r[1, 0:1] + ss_r[2, 0:1])
        tot_col = jnp.sum(jnp.where(eye, jnp.broadcast_to(tot, eye.shape), 0.0), axis=1, keepdims=True)
        inv = lax.rsqrt(tot_col / D + NORM_EPS)
        u_b[...] = (h * inv * g).astype(BF)

    def put_rows(dst, cols, val):
        v = val.astype(BF)
        for r in range(4):
            dst[r // 2, r % 2, :, cols] = v[16 * r:16 * r + 16]

    def a_q(l):
        wait(cp_q(l))
        u = u_b[...]
        for n in range(0, QC, 512):
            put_rows(part_q, slice(n, n + 512), jnp.dot(u, wq_b[:, n:n + 512], preferred_element_type=F32))
        put_rows(part_q, slice(QC, QC + HD), jnp.dot(u, wkv_b[...], preferred_element_type=F32))
        rc(part_q.at[:, 1 - c], rb_q, sp(sem_rb, NCH), dev_p).start()

        @pl.when(l + 1 < L)
        def _():
            start(cp_q(l + 1))

    def b_q():
        rc(part_q.at[:, 1 - c], rb_q, sp(sem_rb, NCH), dev_p).wait()
        s = part_q[1 - cx, c].astype(F32) + rb_q[1 - cx].astype(F32)
        part_q[1 - cx, c] = s.astype(BF)
        rc(part_q.at[1 - cx, c], ib_q, sp(sem_ib, NCH), dev_q).start()

    def c_q():
        rc(part_q.at[1 - cx, c], ib_q, sp(sem_ib, NCH), dev_q).wait()
        z = (part_q[cx, c].astype(F32) + rb_q[cx].astype(F32)) + ib_q[...].astype(F32)
        zq[0] = z[0:8].astype(BF)
        zq[1] = z[8:16].astype(BF)
        rc(zq.at[1 - y], yq.at[y], sp(sem_zq), dev_y).start()
        yq[y] = zq[y]

    def attend(l):
        rc(zq.at[1 - y], yq.at[1 - y], sp(sem_zq), dev_y).wait()
        q0 = yq[0].astype(F32)
        q1 = yq[1].astype(F32)
        k_new = q0[:, QC:]
        v_new = q1[:, QC:]
        knew[l] = k_new.astype(BF)
        vnew[l] = v_new.astype(BF)
        nh = QC // HD
        ns = 8
        heads = [qq[:, h * HD:(h + 1) * HD] for qq in (q0, q1) for h in range(nh)]
        qf = jnp.concatenate(heads, axis=0)
        qb = qf.astype(BF)
        nr = 2 * nh * ns
        pos = lax.broadcasted_iota(jnp.int32, (nr, HD), 1)
        seq = lax.rem(lax.broadcasted_iota(jnp.int32, (nr, HD), 0), ns)
        ln = jnp.zeros((nr, HD), jnp.int32)
        for b in range(ns):
            ln = jnp.where(seq == b, lens[b], ln)
        k_rep = jnp.concatenate([k_new] * (2 * nh), axis=0)
        v_rep = jnp.concatenate([v_new] * (2 * nh), axis=0)
        s_new = jnp.sum(qf * k_rep, axis=1, keepdims=True)
        wait(cp_kv(l))
        s = jnp.zeros((nr, HD), F32)
        for b in range(ns):
            sb = lax.dot_general(qb, k_b[b], (((1,), (1,)), ((), ())), preferred_element_type=F32)
            s = jnp.where(seq == b, sb, s)
        s = jnp.where(pos == ln, s_new, s) * HD ** -0.5
        s = jnp.where(pos <= ln, s, -1e30)
        e = jnp.exp(s - jnp.max(s, axis=1, keepdims=True))
        p = (e / jnp.sum(e, axis=1, keepdims=True)).astype(BF).astype(F32)
        p_new = jnp.sum(jnp.where(pos == ln, p, 0.0), axis=1, keepdims=True)
        p_old = jnp.where(pos == ln, 0.0, p)
        o = p_new * v_rep
        for b in range(ns):
            pb = jnp.where(seq == b, p_old, 0.0).astype(BF)
            o = o + jnp.dot(pb, v_b[b], preferred_element_type=F32)
        for hh in range(2):
            for h in range(nh):
                r0 = (hh * nh + h) * ns
                ob[hh, :, h * HD:(h + 1) * HD] = o[r0:r0 + ns].astype(BF)
        rc(ob.at[1 - y], o_all.at[x, y], sp(sem_oy), dev_y).start()
        o_all[x, y] = ob[y]

        @pl.when(l + 1 < L)
        def _():
            start(cp_kv(l + 1))

    def o_send():
        rc(ob.at[1 - y], o_all.at[x, 1 - y], sp(sem_oy), dev_y).wait()
        rc(o_all.at[x], o_all.at[x], sp(sem_op), dev_p).start()
        rc(o_all.at[x], o_all.at[x], sp(sem_oq), dev_q).start()

    def o_fwd():
        rc(o_all.at[xq], o_all.at[xq], sp(sem_oq), dev_q).wait_recv()
        rc(o_all.at[xq], o_all.at[xq], sp(sem_of), dev_p).start()

    def e_o(l):
        rc(o_all.at[x], o_all.at[xp], sp(sem_op), dev_p).wait()
        rc(o_all.at[xq], o_all.at[xd], sp(sem_of), dev_p).wait()
        rc(o_all.at[x], o_all.at[x], sp(sem_oq), dev_q).wait_send()
        wait(cp_o(l))
        blocks = [o_all[i // 2, i % 2].astype(F32) for i in range(8)]
        lhs = jnp.concatenate(blocks, axis=0).astype(BF)
        for n in range(0, acc.shape[1], 512):
            acc[:, n:n + 512] += jnp.dot(lhs, wo_b[:, n:n + 512], preferred_element_type=F32)

        @pl.when(l + 1 < L)
        def _():
            start(cp_o(l + 1))

    def stage_a(l, j):
        i = l * NCH + j
        s = lax.rem(i, NG)
        wait(cp_gu(i))
        u = u_b[...]
        dst = part.at[j]
        for n in range(0, CH, 512):
            put_rows(dst, slice(n, n + 512), jnp.dot(u, wg_b[s, :, n:n + 512], preferred_element_type=F32))
            put_rows(dst, slice(CH + n, CH + n + 512), jnp.dot(u, wu_b[s, :, n:n + 512], preferred_element_type=F32))
        rc(part.at[j, :, 1 - c], rb.at[j], sp(sem_rb, j), dev_p).start()

        @pl.when(i + NG < L * NCH)
        def _():
            start(cp_gu(i + NG))

    def stage_b(j):
        rc(part.at[j, :, 1 - c], rb.at[j], sp(sem_rb, j), dev_p).wait()
        s = part[j, 1 - cx, c].astype(F32) + rb[j, 1 - cx].astype(F32)
        part[j, 1 - cx, c] = s.astype(BF)
        rc(part.at[j, 1 - cx, c], ib.at[j], sp(sem_ib, j), dev_q).start()

    def stage_c(j):
        rc(part.at[j, 1 - cx, c], ib.at[j], sp(sem_ib, j), dev_q).wait()
        z = (part[j, cx, c].astype(F32) + rb[j, cx].astype(F32)) + ib[j].astype(F32)
        z = z.astype(BF).astype(F32)
        gate, up = z[:, :CH], z[:, CH:]
        m_all[j, x] = (jax.nn.silu(gate) * up).astype(BF)
        rc(m_all.at[j, x], m_all.at[j, x], sp(sem_mq, j), dev_q).start()
        rc(m_all.at[j, x], m_all.at[j, x], sp(sem_mp, j), dev_p).start()

    def stage_d(j):
        rc(m_all.at[j, xq], m_all.at[j, xq], sp(sem_mq, j), dev_q).wait_recv()
        rc(m_all.at[j, xq], m_all.at[j, xq], sp(sem_mf, j), dev_p).start()

    def stage_e(l, j):
        i = l * NCH + j
        s = lax.rem(i, ND)
        rc(m_all.at[j, x], m_all.at[j, xp], sp(sem_mp, j), dev_p).wait()
        rc(m_all.at[j, xq], m_all.at[j, xd], sp(sem_mf, j), dev_p).wait()
        rc(m_all.at[j, x], m_all.at[j, x], sp(sem_mq, j), dev_q).wait_send()
        wait(cp_d(i))
        m = m_all[j].reshape(rows, CH)
        for n in range(0, acc.shape[1], 512):
            acc[:, n:n + 512] += jnp.dot(m, wd_b[s, :, n:n + 512], preferred_element_type=F32)

        @pl.when(i + ND < L * NCH)
        def _():
            start(cp_d(i + ND))

    def layer(l, carry):
        norm(l)
        acc[...] = jnp.zeros_like(acc)
        a_q(l)

        def step(t, carry2):
            @pl.when((l == 0) & (t + 2 < NG))
            def _():
                start(cp_gu(t + 2))

            @pl.when(t < NCH)
            def _():
                stage_a(l, t)

            @pl.when((l == 0) & (t < ND))
            def _():
                start(cp_d(t))

            @pl.when(t == 0)
            def _():
                @pl.when(l == 0)
                def _():
                    start(cp_kv(0))
                b_q()

            @pl.when(t == 1)
            def _():
                @pl.when(l == 0)
                def _():
                    start(cp_o(0))

            @pl.when((t >= LAG_B) & (t < NCH + LAG_B))
            def _():
                stage_b(t - LAG_B)

            @pl.when(t == 2)
            def _():
                c_q()

            @pl.when((t >= LAG_C) & (t < NCH + LAG_C))
            def _():
                stage_c(t - LAG_C)

            @pl.when(t == 4)
            def _():
                attend(l)

            @pl.when(t == 6)
            def _():
                o_send()

            @pl.when((t >= LAG_D) & (t < NCH + LAG_D))
            def _():
                stage_d(t - LAG_D)

            @pl.when(t == 8)
            def _():
                o_fwd()

            @pl.when((t >= LAG_E) & (t < NCH + LAG_E))
            def _():
                stage_e(l, t - LAG_E)

            @pl.when(t == 10)
            def _():
                e_o(l)
            return carry2

        lax.fori_loop(0, NCH + LAG_E, step, 0)

        yx_s[...] = acc[...].astype(BF)
        yx = rc(yx_s, yx_r, sp(sem_yx), dev_y)
        yx.start()
        yx.wait()
        h_b[...] = (h_b[...].astype(F32) + (yx_s[...].astype(F32) + yx_r[...].astype(F32))).astype(BF)
        return carry

    lax.fori_loop(0, L, layer, 0)
    hout[...] = h_b[:, pl.ds(pl.multiple_of(y * half, half), half)]


def solution(mesh):
    row_spec = P("dp", ("x", "yz"))
    tile_in = P(None, "x", "yz")
    tile_out = P(None, "yz", "x")
    cache_spec = P(None, ("dp", "x", "yz"))
    len_spec = P(("dp", "x", "yz"))

    def device_step(hidden, norm_gain, w_q, w_kv, w_gate, w_up, w_o, w_down, k_cache, v_cache, seq_len):
        L, k_in, q_cols = w_q.shape
        rows = hidden.shape[0]
        half = hidden.shape[1]
        kv_cols = w_kv.shape[2]
        ff = w_gate.shape[2]
        ch = 1024
        nch = ff // ch
        d_out = w_o.shape[2]
        ns, cache_len, hd = k_cache.shape[1:]
        zc = q_cols + kv_cols
        dims = {"layers": L, "chunk": ch, "n_chunks": nch, "d": half * 8}
        vm = pl.BlockSpec(memory_space=pltpu.VMEM)
        anyspec = pl.BlockSpec(memory_space=pl.ANY)
        DMA = pltpu.SemaphoreType.DMA
        V = pltpu.VMEM
        h_new, k_new, v_new = pl.pallas_call(
            functools.partial(step_kernel, dims),
            out_shape=(
                jax.ShapeDtypeStruct(hidden.shape, BF),
                jax.ShapeDtypeStruct((L, ns, hd), BF),
                jax.ShapeDtypeStruct((L, ns, hd), BF),
            ),
            in_specs=[vm, vm] + [anyspec] * 8 + [pl.BlockSpec(memory_space=pltpu.SMEM)],
            out_specs=(vm, vm, vm),
            scratch_shapes=[
                V((k_in, q_cols), BF), V((k_in, kv_cols), BF),
                V((NG, k_in, ch), BF), V((NG, k_in, ch), BF),
                V((q_cols, d_out), BF), V((ND, ch, d_out), BF),
                V((ns, cache_len, hd), BF), V((ns, cache_len, hd), BF),
                V((2, rows, half), BF), V((rows, d_out), BF), V((rows, d_out), BF), V((rows, d_out), F32),
                V((8, 128), F32), V((3, 8, 128), F32),
                V((nch, 2, 2, 16, 2 * ch), BF), V((nch, 2, 16, 2 * ch), BF), V((nch, 16, 2 * ch), BF),
                V((nch, 4, 16, ch), BF),
                V((2, 2, 16, zc), BF), V((2, 16, zc), BF), V((16, zc), BF),
                V((2, ns, zc), BF), V((2, ns, zc), BF),
                V((2, ns, q_cols), BF), V((4, 2, ns, q_cols), BF),
                V((rows, d_out), BF), V((rows, d_out), BF),
                DMA, DMA, DMA((NG,)), DMA((NG,)), DMA, DMA((ND,)), DMA, DMA,
                DMA((2,)), DMA((2, 3)), DMA((2, nch + 1)), DMA((2, nch + 1)),
                DMA((2, nch)), DMA((2, nch)), DMA((2, nch)),
                DMA((2,)), DMA((2,)), DMA((2,)), DMA((2,)), DMA((2,)), DMA((2,)),
            ],
            compiler_params=pltpu.CompilerParams(
                collective_id=0, has_side_effects=True, vmem_limit_bytes=67_000_000),
            name="decode_step",
        )(hidden, norm_gain, w_q, w_kv, w_gate, w_up, w_o, w_down, k_cache, v_cache, seq_len)
        slot_hit = (jnp.arange(cache_len)[None, :] == seq_len[:, None])[None, :, :, None]
        k_out = jnp.where(slot_hit, k_new[:, :, None, :], k_cache)
        v_out = jnp.where(slot_hit, v_new[:, :, None, :], v_cache)
        return h_new, k_out, v_out

    return jax.shard_map(
        device_step,
        mesh=mesh,
        in_specs=(row_spec, P(None, "x"), tile_in, tile_in, tile_in, tile_in, tile_out, tile_out, cache_spec, cache_spec, len_spec),
        out_specs=(row_spec, cache_spec, cache_spec),
        check_vma=False,
    )
```

time: 348 us -> 127 us (0.36)
  Pallas kernels: 0 us -> 120 us
  waiting for transfers between devices: 111 us -> 0 us
  matrix products: 104 us -> 0 us
  blocking collectives: 77.1 us -> 0 us
  other arithmetic: 24.1 us -> 5.67 us
  between operations: 14.2 us -> 0.65 us
  starting transfers between devices: 10.3 us -> 0 us
  local copies, waits for them, and re-layouts: 5.12 us -> 0.63 us
    pallas_call x0 -> x1, Pallas kernels: none -> 120 us  [device_step(): pl.pallas_call(functools.partial(step_kernel, dims), out_shape=(jax.Shape...]
    reduce_scatter x6 -> x0, waiting for transfers between devices: 105 us -> none  [the longest x3 84.4 us: device_step(): proj_rows = lax.psum_scatter(part_sum, 'x', scatter_dimension=0, tiled=True)]
    dot_general x24 -> x0, matrix products: 104 us -> none  [the longest x12 58.2 us: device_step(): jnp.dot(normed, weight[layer_idx], preferred_element_type=jnp.float32)]
    all_gather x6 -> x0, blocking collectives: 39.8 us -> none  [the longest x3 23.7 us: device_step(): attn_rows = lax.all_gather(attn_back, 'x', axis=0, tiled=True)]
    all_to_all x3 -> x0, blocking collectives: 19.7 us -> none  [the longest x2 13 us: device_step(): lax.all_to_all(attn_out.reshape(local_seqs, n_heads * head_dim), 'yz', 1,...]
    psum x3 -> x0, blocking collectives: 17.7 us -> none  [device_step(): sq_sum = lax.psum(jnp.sum(feat_f32 * feat_f32, axis=1, keepdims=True), 'x')]
    all_to_all x3 -> x0, starting transfers between devices: 9.91 us -> none  [the longest x2 6.61 us: device_step(): lax.all_to_all(proj_rows[:, :attn_cols], 'yz', 0, 1, tiled=True)]
    convert_element_type x6 -> x0, other arithmetic: 8.86 us -> none  [the longest x3 5.66 us: device_step(): mlp_act = (jax.nn.silu(gate_act) * up_act).astype(jnp.bfloat16)]
  transfers between devices with their start and end apart: 12 -> 0, of which waited for: 8 -> 0; matrix products, arithmetic and copies ran while one was open for 9% -> 0% of each run, Pallas kernels for 0% -> 0%
where the time goes in v1:
time: 127 us
  Pallas kernels  120 us (94%)
  other arithmetic  5.67 us (4%)
    pallas_call x1, Pallas kernels, device_step(): pl.pallas_call(functools.partial(step_kernel, dims), out_shape=(jax.Shape...  120 us
    select_n x1, other arithmetic, device_step(): v_out = jnp.where(slot_hit, v_new[:, :, None, :], v_cache)  4.94 us

profile of v1, /device:TPU:0, one launch (start us, length us, event | category | flops | bytes accessed | tf_op | source)
XLA Modules:
  0.0 127.3 jit_solution(10804474894879930698)
XLA Ops:
  0.6 0.7 iota_compare_fusion
  1.4 120.4 %decode_step.1 = (bf16[64,512]{1,0:T(8,128)(2,1)}, bf16[3,8,256]{2,1,0:T(8,128)(2,1)}, bf16[3,8,256]{2,1,0:T(8,128)(2,1)}) custom-call(bf16[64,512]{1,0:T(8,128)(2,1)} %hid.1, bf16[3,1024]{1,0:T(4,128)(2,1)} %gain.1, bf16[3,1024,2048]{2,1,0:T(8,128)(2,1)} %wq.1, bf16[3,1024,256]{2,1,0:T(8,128)(2,1)} %wkv.1, bf16[3,1024,8192]{2,1,0:T(8,128)(2,1)} %wg.1, ...), custom_call_target="tpu_custom_call" | custom-call | tf_op jit(solution)/shard_map/decode_step/pallas_call | solution.py:375
  121.7 0.0 copy-start
  121.8 4.9 %broadcast_select_fusion = (bf16[3,8,256,256]{3,2,1,0:T(8,128)(2,1)}, bf16[3,8,256,256]{3,2,1,0:T(8,128)(2,1)}) fusion(bf16[3,8,256,256]{3,2,1,0:T(8,128)(2,1)} %vc.1, pred[8,256]{1,0:T(8,128)(4,1)S(1)} %iota_compare_fusion, bf16[3,8,256]{2,1,0:T(8,128)(2,1)} %get-tuple-element.8, bf16[3,8,256,256]{3,2,1,0:T(8,128)(2,1)} %kc.1, ...), kind=kLoop, calls=%fused_computation | loop fusion | flops 3145728 | bytes 12609536 | tf_op jit(solution)/shard_map/jit(_where)/select_n | solution.py:408
  126.7 0.0 copy-done
  126.7 0.6 copy.15
Async XLA Ops:
  121.7 5.0 %copy-start = (bf16[64,512]{1,0:T(8,128)(2,1)S(1)}, bf16[64,512]{1,0:T(8,128)(2,1)}, u32[]{:S(2)}) copy-start(bf16[64,512]{1,0:T(8,128)(2,1)} %get-tuple-element.14) | copy-start | bytes 196612

commit v2 on v1

--- a/solution.py
+++ b/solution.py
@@ -12,9 +12,16 @@
 BF = jnp.bfloat16
 F32 = jnp.float32
 
+CH = 1024
 NG = 7
-ND = 7
-LAG_B, LAG_C, LAG_D, LAG_E = 1, 3, 5, 6
+ND = 8
+T_B = (1, 2, 3, 4, 5, 6, 7, 8)
+T_C = (5, 7, 8, 9, 10, 11, 12, 13)
+T_D = (11, 13, 14, 15, 16, 18, 19)
+T_EN = (8, 9, 10, 11, 12, 13, 14)
+T_EF = (12, 14, 15, 16, 17, 19, 20)
+T_QB, T_QC, T_ATT, T_OS, T_ON, T_OF, T_OE, T_LN = 0, 4, 7, 11, 12, 17, 18, 14
+STEPS = 21
 
 
 def step_kernel(dims, hid, gain, wq, wkv, wg, wu, wo, wd, kc, vc, lens,
@@ -25,7 +32,7 @@
                 sem_wq, sem_wkv, sem_g, sem_u, sem_wo, sem_d, sem_k, sem_v,
                 sem_h, sem_ss, sem_rb, sem_ib, sem_mp, sem_mq, sem_mf,
                 sem_zq, sem_oy, sem_op, sem_oq, sem_of, sem_yx):
-    L, CH, NCH, D = dims["layers"], dims["chunk"], dims["n_chunks"], dims["d"]
+    L, NCH, D = dims["layers"], dims["n_chunks"], dims["d"]
     HD = 256
     QC = wq_b.shape[1]
     x = lax.axis_index("x")
@@ -76,27 +83,33 @@
             cpy.wait()
 
     start(cp_q(0))
-    start(cp_gu(0))
-
-    barrier = pltpu.get_barrier_semaphore()
-    for dev in (dev_p, dev_q, dev_d, dev_y):
-        pl.semaphore_signal(barrier, inc=1, device_id=dev, device_id_type=MESH)
-    pl.semaphore_wait(barrier, 4)
-
-    h_send = rc(hid, hin.at[y], sp(sem_h), dev_y)
-    h_send.start()
-    hin[y] = hid[...]
-    start(cp_gu(1))
-    rc(hid, hin.at[1 - y], sp(sem_h), dev_y).wait_recv()
-    half = hid.shape[1]
-    h_b[:, :half] = hin[0]
-    h_b[:, half:] = hin[1]
-    h_send.wait_send()
+    for k in range(4):
+        start(cp_gu(k))
+
+    with jax.named_scope("barrier"):
+        barrier = pltpu.get_barrier_semaphore()
+        for dev in (dev_p, dev_q, dev_d, dev_y):
+            pl.semaphore_signal(barrier, inc=1, device_id=dev, device_id_type=MESH)
+        pl.semaphore_wait(barrier, 4)
+
+    with jax.named_scope("hx"):
+        h_send = rc(hid, hin.at[y], sp(sem_h), dev_y)
+        h_send.start()
+        for k in range(4, NG):
+            start(cp_gu(k))
+        start(cp_kv(0))
+        hin[y] = hid[...]
+        rc(hid, hin.at[1 - y], sp(sem_h), dev_y).wait_recv()
+        half = hid.shape[1]
+        h_b[:, :half] = hin[0]
+        h_b[:, half:] = hin[1]
+        h_send.wait_send()
 
     rows = h_b.shape[0]
     eye = (lax.broadcasted_iota(jnp.int32, (rows, 128), 0)
            == lax.broadcasted_iota(jnp.int32, (rows, 128), 1))
 
+    @jax.named_scope("norm")
     def norm(l):
         h = h_b[...].astype(F32)
         ss = jnp.sum(h * h, axis=1, keepdims=True)
@@ -122,6 +135,7 @@
         for r in range(4):
             dst[r // 2, r % 2, :, cols] = v[16 * r:16 * r + 16]
 
+    @jax.named_scope("a_q")
     def a_q(l):
         wait(cp_q(l))
         u = u_b[...]
@@ -134,12 +148,14 @@
         def _():
             start(cp_q(l + 1))
 
+    @jax.named_scope("b_q")
     def b_q():
         rc(part_q.at[:, 1 - c], rb_q, sp(sem_rb, NCH), dev_p).wait()
         s = part_q[1 - cx, c].astype(F32) + rb_q[1 - cx].astype(F32)
         part_q[1 - cx, c] = s.astype(BF)
         rc(part_q.at[1 - cx, c], ib_q, sp(sem_ib, NCH), dev_q).start()
 
+    @jax.named_scope("c_q")
     def c_q():
         rc(part_q.at[1 - cx, c], ib_q, sp(sem_ib, NCH), dev_q).wait()
         z = (part_q[cx, c].astype(F32) + rb_q[cx].astype(F32)) + ib_q[...].astype(F32)
@@ -148,6 +164,7 @@
         rc(zq.at[1 - y], yq.at[y], sp(sem_zq), dev_y).start()
         yq[y] = zq[y]
 
+    @jax.named_scope("attend")
     def attend(l):
         rc(zq.at[1 - y], yq.at[1 - y], sp(sem_zq), dev_y).wait()
         q0 = yq[0].astype(F32)
@@ -189,36 +206,47 @@
             for h in range(nh):
                 r0 = (hh * nh + h) * ns
                 ob[hh, :, h * HD:(h + 1) * HD] = o[r0:r0 + ns].astype(BF)
-        rc(ob.at[1 - y], o_all.at[x, y], sp(sem_oy), dev_y).start()
-        o_all[x, y] = ob[y]
+        rc(ob.at[1 - y], o_all.at[cx, c, y], sp(sem_oy), dev_y).start()
+        o_all[cx, c, y] = ob[y]
 
         @pl.when(l + 1 < L)
         def _():
             start(cp_kv(l + 1))
 
+    @jax.named_scope("o_send")
     def o_send():
-        rc(ob.at[1 - y], o_all.at[x, 1 - y], sp(sem_oy), dev_y).wait()
-        rc(o_all.at[x], o_all.at[x], sp(sem_op), dev_p).start()
-        rc(o_all.at[x], o_all.at[x], sp(sem_oq), dev_q).start()
-
+        rc(ob.at[1 - y], o_all.at[cx, c, 1 - y], sp(sem_oy), dev_y).wait()
+        rc(o_all.at[cx, c], o_all.at[cx, c], sp(sem_op), dev_p).start()
+        rc(o_all.at[cx, c], o_all.at[cx, c], sp(sem_oq), dev_q).start()
+
+    @jax.named_scope("o_fwd")
     def o_fwd():
-        rc(o_all.at[xq], o_all.at[xq], sp(sem_oq), dev_q).wait_recv()
-        rc(o_all.at[xq], o_all.at[xq], sp(sem_of), dev_p).start()
-
-    def e_o(l):
-        rc(o_all.at[x], o_all.at[xp], sp(sem_op), dev_p).wait()
-        rc(o_all.at[xq], o_all.at[xd], sp(sem_of), dev_p).wait()
-        rc(o_all.at[x], o_all.at[x], sp(sem_oq), dev_q).wait_send()
+        rc(o_all.at[1 - cx, c], o_all.at[1 - cx, c], sp(sem_oq), dev_q).wait_recv()
+        rc(o_all.at[1 - cx, c], o_all.at[1 - cx, c], sp(sem_of), dev_p).start()
+
+    def o_rows(g):
+        blocks = [o_all[g, i // 2, i % 2].astype(F32) for i in range(4)]
+        lhs = jnp.concatenate(blocks, axis=0).astype(BF)
+        for n in range(0, acc.shape[2], 512):
+            acc[g, :, n:n + 512] += jnp.dot(lhs, wo_b[:, n:n + 512], preferred_element_type=F32)
+
+    @jax.named_scope("o_near")
+    def o_near(l):
+        rc(o_all.at[cx, c], o_all.at[cx, 1 - c], sp(sem_op), dev_p).wait()
         wait(cp_o(l))
-        blocks = [o_all[i // 2, i % 2].astype(F32) for i in range(8)]
-        lhs = jnp.concatenate(blocks, axis=0).astype(BF)
-        for n in range(0, acc.shape[1], 512):
-            acc[:, n:n + 512] += jnp.dot(lhs, wo_b[:, n:n + 512], preferred_element_type=F32)
+        o_rows(cx)
+
+    @jax.named_scope("o_far")
+    def o_far(l):
+        rc(o_all.at[1 - cx, c], o_all.at[1 - cx, 1 - c], sp(sem_of), dev_p).wait()
+        rc(o_all.at[cx, c], o_all.at[cx, c], sp(sem_oq), dev_q).wait_send()
+        o_rows(1 - cx)
 
         @pl.when(l + 1 < L)
         def _():
             start(cp_o(l + 1))
 
+    @jax.named_scope("stage_a")
     def stage_a(l, j):
         i = l * NCH + j
         s = lax.rem(i, NG)
@@ -234,35 +262,46 @@
         def _():
             start(cp_gu(i + NG))
 
+    @jax.named_scope("stage_b")
     def stage_b(j):
         rc(part.at[j, :, 1 - c], rb.at[j], sp(sem_rb, j), dev_p).wait()
         s = part[j, 1 - cx, c].astype(F32) + rb[j, 1 - cx].astype(F32)
         part[j, 1 - cx, c] = s.astype(BF)
         rc(part.at[j, 1 - cx, c], ib.at[j], sp(sem_ib, j), dev_q).start()
 
+    @jax.named_scope("stage_c")
     def stage_c(j):
         rc(part.at[j, 1 - cx, c], ib.at[j], sp(sem_ib, j), dev_q).wait()
         z = (part[j, cx, c].astype(F32) + rb[j, cx].astype(F32)) + ib[j].astype(F32)
         z = z.astype(BF).astype(F32)
         gate, up = z[:, :CH], z[:, CH:]
-        m_all[j, x] = (jax.nn.silu(gate) * up).astype(BF)
-        rc(m_all.at[j, x], m_all.at[j, x], sp(sem_mq, j), dev_q).start()
-        rc(m_all.at[j, x], m_all.at[j, x], sp(sem_mp, j), dev_p).start()
-
+        m_all[j, cx, c] = (jax.nn.silu(gate) * up).astype(BF)
+        rc(m_all.at[j, cx, c], m_all.at[j, cx, c], sp(sem_mq, j), dev_q).start()
+        rc(m_all.at[j, cx, c], m_all.at[j, cx, c], sp(sem_mp, j), dev_p).start()
+
+    @jax.named_scope("stage_d")
     def stage_d(j):
-        rc(m_all.at[j, xq], m_all.at[j, xq], sp(sem_mq, j), dev_q).wait_recv()
-        rc(m_all.at[j, xq], m_all.at[j, xq], sp(sem_mf, j), dev_p).start()
-
-    def stage_e(l, j):
+        rc(m_all.at[j, 1 - cx, c], m_all.at[j, 1 - cx, c], sp(sem_mq, j), dev_q).wait_recv()
+        rc(m_all.at[j, 1 - cx, c], m_all.at[j, 1 - cx, c], sp(sem_mf, j), dev_p).start()
+
+    def e_rows(s, j, g):
+        m = m_all[j, g].reshape(rows // 2, CH)
+        for n in range(0, acc.shape[2], 512):
+            acc[g, :, n:n + 512] += jnp.dot(m, wd_b[s, :, n:n + 512], preferred_element_type=F32)
+
+    @jax.named_scope("e_near")
+    def e_near(l, j):
         i = l * NCH + j
-        s = lax.rem(i, ND)
-        rc(m_all.at[j, x], m_all.at[j, xp], sp(sem_mp, j), dev_p).wait()
-        rc(m_all.at[j, xq], m_all.at[j, xd], sp(sem_mf, j), dev_p).wait()
-        rc(m_all.at[j, x], m_all.at[j, x], sp(sem_mq, j), dev_q).wait_send()
+        rc(m_all.at[j, cx, c], m_all.at[j, cx, 1 - c], sp(sem_mp, j), dev_p).wait()
         wait(cp_d(i))
-        m = m_all[j].reshape(rows, CH)
-        for n in range(0, acc.shape[1], 512):
-            acc[:, n:n + 512] += jnp.dot(m, wd_b[s, :, n:n + 512], preferred_element_type=F32)
+        e_rows(lax.rem(i, ND), j, cx)
+
+    @jax.named_scope("e_far")
+    def e_far(l, j):
+        i = l * NCH + j
+        rc(m_all.at[j, 1 - cx, c], m_all.at[j, 1 - cx, 1 - c], sp(sem_mf, j), dev_p).wait()
+        rc(m_all.at[j, cx, c], m_all.at[j, cx, c], sp(sem_mq, j), dev_q).wait_send()
+        e_rows(lax.rem(i, ND), j, 1 - cx)
 
         @pl.when(i + ND < L * NCH)
         def _():
@@ -274,76 +313,84 @@
         a_q(l)
 
         def step(t, carry2):
-            @pl.when((l == 0) & (t + 2 < NG))
-            def _():
-                start(cp_gu(t + 2))
-
-            @pl.when(t < NCH)
-            def _():
-                stage_a(l, t)
-
-            @pl.when((l == 0) & (t < ND))
-            def _():
-                start(cp_d(t))
-
-            @pl.when(t == 0)
-            def _():
-                @pl.when(l == 0)
-                def _():
-                    start(cp_kv(0))
-                b_q()
-
-            @pl.when(t == 1)
-            def _():
-                @pl.when(l == 0)
-                def _():
-                    start(cp_o(0))
-
-            @pl.when((t >= LAG_B) & (t < NCH + LAG_B))
-            def _():
-                stage_b(t - LAG_B)
-
-            @pl.when(t == 2)
-            def _():
-                c_q()
-
-            @pl.when((t >= LAG_C) & (t < NCH + LAG_C))
-            def _():
-                stage_c(t - LAG_C)
-
-            @pl.when(t == 4)
-            def _():
-                attend(l)
-
-            @pl.when(t == 6)
-            def _():
-                o_send()
-
-            @pl.when((t >= LAG_D) & (t < NCH + LAG_D))
-            def _():
-                stage_d(t - LAG_D)
-
-            @pl.when(t == 8)
-            def _():
-                o_fwd()
-
-            @pl.when((t >= LAG_E) & (t < NCH + LAG_E))
-            def _():
-                stage_e(l, t - LAG_E)
-
-            @pl.when(t == 10)
-            def _():
-                e_o(l)
+            def at(steps, fn):
+                if isinstance(steps, int):
+                    pl.when(t == steps)(fn)
+                    return
+                hit = t == steps[0]
+                j = jnp.int32(0)
+                for k, st in enumerate(steps[1:]):
+                    hit = hit | (t == st)
+                    j = jnp.where(t >= st, k + 1, j)
+                pl.when(hit)(lambda: fn(j))
+
+            pl.when(t < NCH)(lambda: stage_a(l, t))
+            pl.when((l == 0) & (t < ND))(lambda: start(cp_d(t)))
+            pl.when((l == 0) & (t == 3))(lambda: start(cp_o(0)))
+            at(T_QB, b_q)
+            at(T_B, stage_b)
+            at(T_QC, c_q)
+            at(T_EN, lambda j: e_near(l, j))
+            at(T_OS, o_send)
+            at(T_D, stage_d)
+            at(T_ON, lambda: o_near(l))
+            at(T_OE, lambda: o_far(l))
+            at(T_EF, lambda j: e_far(l, j))
+            at(T_OF, o_fwd)
+            at(T_C, stage_c)
+            at(T_ATT, lambda: attend(l))
+            at(T_LN, lambda: last_near(l))
             return carry2
 
-        lax.fori_loop(0, NCH + LAG_E, step, 0)
-
-        yx_s[...] = acc[...].astype(BF)
-        yx = rc(yx_s, yx_r, sp(sem_yx), dev_y)
-        yx.start()
-        yx.wait()
-        h_b[...] = (h_b[...].astype(F32) + (yx_s[...].astype(F32) + yx_r[...].astype(F32))).astype(BF)
+        lax.fori_loop(0, STEPS, step, 0)
+
+        stage_d(NCH - 1)
+        last_far(l)
+        swap(l)
         return carry
+
+    def yx(g, n):
+        return rc(yx_s.at[g, n], yx_r.at[g, n], sp(sem_yx, g, n), dev_y)
+
+    def last_rows(s, g):
+        m = m_all[NCH - 1, g].reshape(rows // 2, CH)
+        for n in range(2):
+            cols = slice(n * half, (n + 1) * half)
+            v = acc[g, :, cols] + jnp.dot(m, wd_b[s, :, cols], preferred_element_type=F32)
+            yx_s[g, n] = v.astype(BF)
+            yx(g, n).start()
+
+    @jax.named_scope("last_near")
+    def last_near(l):
+        j = NCH - 1
+        i = l * NCH + j
+        rc(m_all.at[j, cx, c], m_all.at[j, cx, 1 - c], sp(sem_mp, j), dev_p).wait()
+        wait(cp_d(i))
+        last_rows(lax.rem(i, ND), cx)
+
+    @jax.named_scope("last_far")
+    def last_far(l):
+        j = NCH - 1
+        i = l * NCH + j
+        rc(m_all.at[j, 1 - cx, c], m_all.at[j, 1 - cx, 1 - c], sp(sem_mf, j), dev_p).wait()
+        last_rows(lax.rem(i, ND), 1 - cx)
+
+        @pl.when(i + ND < L * NCH)
+        def _():
+            start(cp_d(i + ND))
+
+    @jax.named_scope("swap")
+    def swap(l):
+        rc(m_all.at[NCH - 1, cx, c], m_all.at[NCH - 1, cx, c], sp(sem_mq, NCH - 1), dev_q).wait_send()
+        for g in (cx, 1 - cx):
+            for n in range(2):
+                yx(g, n).wait()
+        hr = rows // 2
+        for g in range(2):
+            for n in range(2):
+                rr, cc = slice(g * hr, (g + 1) * hr), slice(n * half, (n + 1) * half)
+                upd = yx_s[g, n].astype(F32) + yx_r[g, n].astype(F32)
+                h_b[rr, cc] = (h_b[rr, cc].astype(F32) + upd).astype(BF)
 
     lax.fori_loop(0, L, layer, 0)
     hout[...] = h_b[:, pl.ds(pl.multiple_of(y * half, half), half)]
@@ -362,12 +409,12 @@
         half = hidden.shape[1]
         kv_cols = w_kv.shape[2]
         ff = w_gate.shape[2]
-        ch = 1024
+        ch = CH
         nch = ff // ch
         d_out = w_o.shape[2]
         ns, cache_len, hd = k_cache.shape[1:]
         zc = q_cols + kv_cols
-        dims = {"layers": L, "chunk": ch, "n_chunks": nch, "d": half * 8}
+        dims = {"layers": L, "n_chunks": nch, "d": half * 8}
         vm = pl.BlockSpec(memory_space=pltpu.VMEM)
         anyspec = pl.BlockSpec(memory_space=pl.ANY)
         DMA = pltpu.SemaphoreType.DMA
@@ -386,18 +433,18 @@
                 V((NG, k_in, ch), BF), V((NG, k_in, ch), BF),
                 V((q_cols, d_out), BF), V((ND, ch, d_out), BF),
                 V((ns, cache_len, hd), BF), V((ns, cache_len, hd), BF),
-                V((2, rows, half), BF), V((rows, d_out), BF), V((rows, d_out), BF), V((rows, d_out), F32),
+                V((2, rows, half), BF), V((rows, d_out), BF), V((rows, d_out), BF), V((2, rows // 2, d_out), F32),
                 V((8, 128), F32), V((3, 8, 128), F32),
                 V((nch, 2, 2, 16, 2 * ch), BF), V((nch, 2, 16, 2 * ch), BF), V((nch, 16, 2 * ch), BF),
-                V((nch, 4, 16, ch), BF),
+                V((nch, 2, 2, 16, ch), BF),
                 V((2, 2, 16, zc), BF), V((2, 16, zc), BF), V((16, zc), BF),
                 V((2, ns, zc), BF), V((2, ns, zc), BF),
-                V((2, ns, q_cols), BF), V((4, 2, ns, q_cols), BF),
-                V((rows, d_out), BF), V((rows, d_out), BF),
+                V((2, ns, q_cols), BF), V((2, 2, 2, ns, q_cols), BF),
+                V((2, 2, rows // 2, half), BF), V((2, 2, rows // 2, half), BF),
                 DMA, DMA, DMA((NG,)), DMA((NG,)), DMA, DMA((ND,)), DMA, DMA,
                 DMA((2,)), DMA((2, 3)), DMA((2, nch + 1)), DMA((2, nch + 1)),
                 DMA((2, nch)), DMA((2, nch)), DMA((2, nch)),
-                DMA((2,)), DMA((2,)), DMA((2,)), DMA((2,)), DMA((2,)), DMA((2,)),
+                DMA((2,)), DMA((2,)), DMA((2,)), DMA((2,)), DMA((2,)), DMA((2, 2, 2)),
             ],
             compiler_params=pltpu.CompilerParams(
                 collective_id=0, has_side_effects=True, vmem_limit_bytes=67_000_000),

time: 127 us -> 118 us (0.929)
  Pallas kernels: 120 us -> 111 us
    pallas_call x1, Pallas kernels: 120 us -> 111 us  [device_step(): pl.pallas_call(functools.partial(step_kernel, dims), out_shape=(jax.Shape...]
where the time goes in v2:
time: 118 us
  Pallas kernels  111 us (94%)
  other arithmetic  5.67 us (5%)
    pallas_call x1, Pallas kernels, device_step(): pl.pallas_call(functools.partial(step_kernel, dims), out_shape=(jax.Shape...  111 us
    select_n x1, other arithmetic, device_step(): v_out = jnp.where(slot_hit, v_new[:, :, None, :], v_cache)  4.94 us

profile of v2, /device:TPU:0, one launch (start us, length us, event | category | flops | bytes accessed | tf_op | source)
XLA Modules:
  0.0 117.7 jit_solution(16648422496765736171)
XLA Ops:
  0.6 0.7 iota_compare_fusion
  1.4 110.7 %decode_step.1 = (bf16[64,512]{1,0:T(8,128)(2,1)}, bf16[3,8,256]{2,1,0:T(8,128)(2,1)}, bf16[3,8,256]{2,1,0:T(8,128)(2,1)}) custom-call(bf16[64,512]{1,0:T(8,128)(2,1)} %hid.1, bf16[3,1024]{1,0:T(4,128)(2,1)} %gain.1, bf16[3,1024,2048]{2,1,0:T(8,128)(2,1)} %wq.1, bf16[3,1024,256]{2,1,0:T(8,128)(2,1)} %wkv.1, bf16[3,1024,8192]{2,1,0:T(8,128)(2,1)} %wg.1, ...), custom_call_target="tpu_custom_call" | custom-call | tf_op jit(solution)/shard_map/decode_step/pallas_call | solution.py:422
  112.1 0.0 copy-start
  112.1 4.9 %broadcast_select_fusion = (bf16[3,8,256,256]{3,2,1,0:T(8,128)(2,1)}, bf16[3,8,256,256]{3,2,1,0:T(8,128)(2,1)}) fusion(bf16[3,8,256,256]{3,2,1,0:T(8,128)(2,1)} %vc.1, pred[8,256]{1,0:T(8,128)(4,1)S(1)} %iota_compare_fusion, bf16[3,8,256]{2,1,0:T(8,128)(2,1)} %get-tuple-element.8, bf16[3,8,256,256]{3,2,1,0:T(8,128)(2,1)} %kc.1, ...), kind=kLoop, calls=%fused_computation | loop fusion | flops 3145728 | bytes 12609536 | tf_op jit(solution)/shard_map/jit(_where)/select_n | solution.py:455
  117.0 0.0 copy-done
  117.0 0.6 copy.15
Async XLA Ops:
  112.1 5.0 %copy-start = (bf16[64,512]{1,0:T(8,128)(2,1)S(1)}, bf16[64,512]{1,0:T(8,128)(2,1)}, u32[]{:S(2)}) copy-start(bf16[64,512]{1,0:T(8,128)(2,1)} %get-tuple-element.14) | copy-start | bytes 196612

commit v3 on v2

--- a/solution.py
+++ b/solution.py
@@ -16,21 +16,21 @@
 NG = 7
 ND = 8
 T_B = (1, 2, 3, 4, 5, 6, 7, 8)
-T_C = (5, 7, 8, 9, 10, 11, 12, 13)
-T_D = (11, 13, 14, 15, 16, 18, 19)
+T_C = (4, 6, 8, 9, 10, 11, 12, 14)
+T_D = (10, 12, 15, 16, 17, 18, 19)
 T_EN = (8, 9, 10, 11, 12, 13, 14)
-T_EF = (12, 14, 15, 16, 17, 19, 20)
-T_QB, T_QC, T_ATT, T_OS, T_ON, T_OF, T_OE, T_LN = 0, 4, 7, 11, 12, 17, 18, 14
-STEPS = 21
+T_EF = (12, 14, 17, 18, 19, 20, 21)
+T_QB, T_QC, T_ATT, T_OS, T_ON, T_OF, T_OE, T_LN = 0, 2, 5, 8, 10, 14, 16, 15
+STEPS = 22
 
 
 def step_kernel(dims, hid, gain, wq, wkv, wg, wu, wo, wd, kc, vc, lens,
                 hout, knew, vnew,
                 wq_b, wkv_b, wg_b, wu_b, wo_b, wd_b, k_b, v_b,
-                hin, h_b, u_b, acc, ss_s, ss_r,
+                hin, h_b, u_b, acc, ss_s, ss_r, ss0, tot,
                 part, rb, ib, m_all, part_q, rb_q, ib_q, zq, yq, ob, o_all, yx_s, yx_r,
                 sem_wq, sem_wkv, sem_g, sem_u, sem_wo, sem_d, sem_k, sem_v,
-                sem_h, sem_ss, sem_rb, sem_ib, sem_mp, sem_mq, sem_mf,
+                sem_h, sem_s0, sem_ss, sem_rb, sem_ib, sem_mp, sem_mq, sem_mf,
                 sem_zq, sem_oy, sem_op, sem_oq, sem_of, sem_yx):
     L, NCH, D = dims["layers"], dims["n_chunks"], dims["d"]
     HD = 256
@@ -86,15 +86,33 @@
     for k in range(4):
         start(cp_gu(k))
 
+    rows = hid.shape[0]
+    eye = (lax.broadcasted_iota(jnp.int32, (rows, 128), 0)
+           == lax.broadcasted_iota(jnp.int32, (rows, 128), 1))
+
+    def row_sums(h):
+        ss = jnp.sum(h * h, axis=1, keepdims=True)
+        row = jnp.sum(jnp.where(eye, ss, 0.0), axis=0, keepdims=True)
+        return jnp.broadcast_to(row, tot.shape)
+
+    me = x * 2 + y
+    ss0[me] = row_sums(hid[...].astype(F32))
+
+    def other(k):
+        return {"x": lax.rem(x + k // 2, 4), "yz": lax.rem(y + k % 2, 2)}
+
     with jax.named_scope("barrier"):
         barrier = pltpu.get_barrier_semaphore()
-        for dev in (dev_p, dev_q, dev_d, dev_y):
-            pl.semaphore_signal(barrier, inc=1, device_id=dev, device_id_type=MESH)
-        pl.semaphore_wait(barrier, 4)
+        for k in range(1, 8):
+            pl.semaphore_signal(barrier, inc=1, device_id=other(k), device_id_type=MESH)
+        pl.semaphore_wait(barrier, 7)
 
     with jax.named_scope("hx"):
         h_send = rc(hid, hin.at[y], sp(sem_h), dev_y)
         h_send.start()
+        s0 = [rc(ss0.at[me], ss0.at[me], sp(sem_s0, k), other(k)) for k in range(1, 8)]
+        for cpy in s0:
+            cpy.start()
         for k in range(4, NG):
             start(cp_gu(k))
         start(cp_kv(0))
@@ -104,60 +122,79 @@
         h_b[:, :half] = hin[0]
         h_b[:, half:] = hin[1]
         h_send.wait_send()
-
-    rows = h_b.shape[0]
-    eye = (lax.broadcasted_iota(jnp.int32, (rows, 128), 0)
-           == lax.broadcasted_iota(jnp.int32, (rows, 128), 1))
-
-    @jax.named_scope("norm")
-    def norm(l):
-        h = h_b[...].astype(F32)
-        ss = jnp.sum(h * h, axis=1, keepdims=True)
-        ss_row = jnp.sum(jnp.where(eye, ss, 0.0), axis=0, keepdims=True)
-        ss_s[...] = jnp.broadcast_to(ss_row, ss_s.shape)
+        for cpy in s0:
+            cpy.wait_send()
+        for k in range(1, 8):
+            frm = lax.rem(x + 4 - k // 2, 4) * 2 + lax.rem(y + 2 - k % 2, 2)
+            rc(ss0.at[frm], ss0.at[frm], sp(sem_s0, k), other(k)).wait_recv()
+        total = ss0[0]
+        for k in range(1, 8):
+            total = total + ss0[k]
+        tot[...] = total
+
+    def norm_exchange():
+        ss_s[...] = row_sums(h_b[...].astype(F32))
         cps = [rc(ss_s, ss_r.at[k], sp(sem_ss, k), dev)
                for k, dev in enumerate((dev_p, dev_q, dev_d))]
         for cpy in cps:
             cpy.start()
+        for cpy in cps:
+            cpy.wait()
+        tot[...] = (ss_s[...] + ss_r[0]) + (ss_r[1] + ss_r[2])
+
+    @jax.named_scope("norm")
+    def norm(l):
+        pl.when(l > 0)(norm_exchange)
         gall = gain[...].astype(F32)
         g = gall[0:1]
         for k in range(1, L):
             g = jnp.where(l == k, gall[k:k + 1], g)
-        for cpy in cps:
-            cpy.wait()
-        tot = (ss_s[0:1] + ss_r[0, 0:1]) + (ss_r[1, 0:1] + ss_r[2, 0:1])
-        tot_col = jnp.sum(jnp.where(eye, jnp.broadcast_to(tot, eye.shape), 0.0), axis=1, keepdims=True)
+        tot_col = jnp.sum(jnp.where(eye, jnp.broadcast_to(tot[0:1], eye.shape), 0.0), axis=1, keepdims=True)
         inv = lax.rsqrt(tot_col / D + NORM_EPS)
-        u_b[...] = (h * inv * g).astype(BF)
+        u_b[...] = (h_b[...].astype(F32) * inv * g).astype(BF)
 
     def put_rows(dst, cols, val):
         v = val.astype(BF)
         for r in range(4):
             dst[r // 2, r % 2, :, cols] = v[16 * r:16 * r + 16]
 
+    pieces = (slice(0, QC // 2), slice(QC // 2, QC + HD))
+
+    def to_p_q(k):
+        cols = pieces[k]
+        return rc(part_q.at[:, 1 - c, :, cols], rb_q.at[:, :, cols], sp(sem_rb, NCH + k), dev_p)
+
+    def to_q_q(k):
+        cols = pieces[k]
+        return rc(part_q.at[1 - cx, c, :, cols], ib_q.at[:, cols], sp(sem_ib, NCH + k), dev_q)
+
     @jax.named_scope("a_q")
     def a_q(l):
         wait(cp_q(l))
         u = u_b[...]
-        for n in range(0, QC, 512):
-            put_rows(part_q, slice(n, n + 512), jnp.dot(u, wq_b[:, n:n + 512], preferred_element_type=F32))
-        put_rows(part_q, slice(QC, QC + HD), jnp.dot(u, wkv_b[...], preferred_element_type=F32))
-        rc(part_q.at[:, 1 - c], rb_q, sp(sem_rb, NCH), dev_p).start()
+        for k in range(2):
+            for n in range(k * QC // 2, (k + 1) * QC // 2, 512):
+                put_rows(part_q, slice(n, n + 512), jnp.dot(u, wq_b[:, n:n + 512], preferred_element_type=F32))
+            if k == 1:
+                put_rows(part_q, slice(QC, QC + HD), jnp.dot(u, wkv_b[...], preferred_element_type=F32))
+            to_p_q(k).start()
 
         @pl.when(l + 1 < L)
         def _():
             start(cp_q(l + 1))
 
     @jax.named_scope("b_q")
-    def b_q():
-        rc(part_q.at[:, 1 - c], rb_q, sp(sem_rb, NCH), dev_p).wait()
-        s = part_q[1 - cx, c].astype(F32) + rb_q[1 - cx].astype(F32)
-        part_q[1 - cx, c] = s.astype(BF)
-        rc(part_q.at[1 - cx, c], ib_q, sp(sem_ib, NCH), dev_q).start()
+    def b_q(k):
+        cols = pieces[k]
+        to_p_q(k).wait()
+        s = part_q[1 - cx, c, :, cols].astype(F32) + rb_q[1 - cx, :, cols].astype(F32)
+        part_q[1 - cx, c, :, cols] = s.astype(BF)
+        to_q_q(k).start()
 
     @jax.named_scope("c_q")
     def c_q():
-        rc(part_q.at[1 - cx, c], ib_q, sp(sem_ib, NCH), dev_q).wait()
+        for k in range(2):
+            to_q_q(k).wait()
         z = (part_q[cx, c].astype(F32) + rb_q[cx].astype(F32)) + ib_q[...].astype(F32)
         zq[0] = z[0:8].astype(BF)
         zq[1] = z[8:16].astype(BF)
@@ -277,6 +314,11 @@
         gate, up = z[:, :CH], z[:, CH:]
         m_all[j, cx, c] = (jax.nn.silu(gate) * up).astype(BF)
         rc(m_all.at[j, cx, c], m_all.at[j, cx, c], sp(sem_mq, j), dev_q).start()
+
+        @pl.when(j == NCH - 1)
+        def _():
+            rc(m_all.at[j, cx, c], m_all.at[j, cx, c], sp(sem_mf, j), dev_d).start()
+
         rc(m_all.at[j, cx, c], m_all.at[j, cx, c], sp(sem_mp, j), dev_p).start()
 
     @jax.named_scope("stage_d")
@@ -311,6 +353,7 @@
         norm(l)
         acc[...] = jnp.zeros_like(acc)
         a_q(l)
+        b_q(0)
 
         def step(t, carry2):
             def at(steps, fn):
@@ -327,24 +370,23 @@
             pl.when(t < NCH)(lambda: stage_a(l, t))
             pl.when((l == 0) & (t < ND))(lambda: start(cp_d(t)))
             pl.when((l == 0) & (t == 3))(lambda: start(cp_o(0)))
-            at(T_QB, b_q)
+            at(T_QB, lambda: b_q(1))
             at(T_B, stage_b)
             at(T_QC, c_q)
+            at(T_OS, o_send)
+            at(T_LN, lambda: last_near(l))
+            at(T_D, stage_d)
             at(T_EN, lambda j: e_near(l, j))
-            at(T_OS, o_send)
-            at(T_D, stage_d)
             at(T_ON, lambda: o_near(l))
             at(T_OE, lambda: o_far(l))
             at(T_EF, lambda j: e_far(l, j))
+            at(T_C, stage_c)
             at(T_OF, o_fwd)
-            at(T_C, stage_c)
             at(T_ATT, lambda: attend(l))
-            at(T_LN, lambda: last_near(l))
             return carry2
 
         lax.fori_loop(0, STEPS, step, 0)
 
-        stage_d(NCH - 1)
         last_far(l)
         swap(l)
         return carry
@@ -352,13 +394,16 @@
     def yx(g, n):
         return rc(yx_s.at[g, n], yx_r.at[g, n], sp(sem_yx, g, n), dev_y)
 
-    def last_rows(s, g):
+    def last_rows(l, s, g):
         m = m_all[NCH - 1, g].reshape(rows // 2, CH)
-        for n in range(2):
-            cols = slice(n * half, (n + 1) * half)
+        for n in (1 - y, y):
+            cols = pl.ds(pl.multiple_of(n * half, half), half)
             v = acc[g, :, cols] + jnp.dot(m, wd_b[s, :, cols], preferred_element_type=F32)
             yx_s[g, n] = v.astype(BF)
-            yx(g, n).start()
+            if n is y:
+                pl.when(l + 1 < L)(lambda: yx(g, y).start())
+            else:
+                yx(g, n).start()
 
     @jax.named_scope("last_near")
     def last_near(l):
@@ -366,14 +411,15 @@
         i = l * NCH + j
         rc(m_all.at[j, cx, c], m_all.at[j, cx, 1 - c], sp(sem_mp, j), dev_p).wait()
         wait(cp_d(i))
-        last_rows(lax.rem(i, ND), cx)
+        last_rows(l, lax.rem(i, ND), cx)
 
     @jax.named_scope("last_far")
     def last_far(l):
         j = NCH - 1
         i = l * NCH + j
-        rc(m_all.at[j, 1 - cx, c], m_all.at[j, 1 - cx, 1 - c], sp(sem_mf, j), dev_p).wait()
-        last_rows(lax.rem(i, ND), 1 - cx)
+        rc(m_all.at[j, cx, c], m_all.at[j, 1 - cx, c], sp(sem_mq, j), dev_q).wait_recv()
+        rc(m_all.at[j, cx, c], m_all.at[j, 1 - cx, 1 - c], sp(sem_mf, j), dev_d).wait_recv()
+        last_rows(l, lax.rem(i, ND), 1 - cx)
 
         @pl.when(i + ND < L * NCH)
         def _():
@@ -382,9 +428,17 @@
     @jax.named_scope("swap")
     def swap(l):
         rc(m_all.at[NCH - 1, cx, c], m_all.at[NCH - 1, cx, c], sp(sem_mq, NCH - 1), dev_q).wait_send()
+        rc(m_all.at[NCH - 1, cx, c], m_all.at[NCH - 1, cx, c], sp(sem_mf, NCH - 1), dev_d).wait_send()
         for g in (cx, 1 - cx):
-            for n in range(2):
-                yx(g, n).wait()
+            yx(g, y).wait_recv()
+            yx(g, 1 - y).wait_send()
+
+        @pl.when(l + 1 < L)
+        def _():
+            for g in (cx, 1 - cx):
+                yx(g, 1 - y).wait_recv()
+                yx(g, y).wait_send()
+
         hr = rows // 2
         for g in range(2):
             for n in range(2):
@@ -394,6 +448,34 @@
 
     lax.fori_loop(0, L, layer, 0)
     hout[...] = h_b[:, pl.ds(pl.multiple_of(y * half, half), half)]
+
+
+def place_kernel(kn, vn, hn, kc, vc, lens, ko, vo, ho, new_b, h_b, kv_b, sem_n, sem_h, sem_in, sem_out):
+    L, ns, _, hd = kc.shape
+    T = 16
+    pairs = [(a, l) for l in range(L) for a in range(2)]
+    news = [pltpu.make_async_copy((kn, vn)[a], new_b.at[a], sem_n.at[a]) for a in range(2)]
+    h_in = pltpu.make_async_copy(hn, h_b, sem_h)
+    ins = [pltpu.make_async_copy((kc, vc)[a].at[l], kv_b.at[a, l], sem_in.at[a, l]) for a, l in pairs]
+    outs = [pltpu.make_async_copy(kv_b.at[a, l], (ko, vo)[a].at[l], sem_out.at[a, l]) for a, l in pairs]
+    for cpy in news + ins + [h_in]:
+        cpy.start()
+    for cpy in news:
+        cpy.wait()
+    row = lax.broadcasted_iota(jnp.int32, (T, hd), 0)
+    for k, (a, l) in enumerate(pairs):
+        ins[k].wait()
+        for b in range(ns):
+            base = pl.multiple_of(lens[b] // T * T, T)
+            tile = kv_b[a, l, b, pl.ds(base, T), :].astype(F32)
+            new = new_b[a, l, b:b + 1, :].astype(F32)
+            kv_b[a, l, b, pl.ds(base, T), :] = jnp.where(row == lens[b] - base, new, tile).astype(BF)
+        outs[k].start()
+    h_in.wait()
+    h_out = pltpu.make_async_copy(h_b, ho, sem_h)
+    h_out.start()
+    for cpy in outs + [h_out]:
+        cpy.wait()
 
 
 def solution(mesh):
@@ -434,7 +516,7 @@
                 V((q_cols, d_out), BF), V((ND, ch, d_out), BF),
                 V((ns, cache_len, hd), BF), V((ns, cache_len, hd), BF),
                 V((2, rows, half), BF), V((rows, d_out), BF), V((rows, d_out), BF), V((2, rows // 2, d_out), F32),
-                V((8, 128), F32), V((3, 8, 128), F32),
+                V((8, 128), F32), V((3, 8, 128), F32), V((8, 8, 128), F32), V((8, 128), F32),
                 V((nch, 2, 2, 16, 2 * ch), BF), V((nch, 2, 16, 2 * ch), BF), V((nch, 16, 2 * ch), BF),
                 V((nch, 2, 2, 16, ch), BF),
                 V((2, 2, 16, zc), BF), V((2, 16, zc), BF), V((16, zc), BF),
@@ -442,7 +524,7 @@
                 V((2, ns, q_cols), BF), V((2, 2, 2, ns, q_cols), BF),
                 V((2, 2, rows // 2, half), BF), V((2, 2, rows // 2, half), BF),
                 DMA, DMA, DMA((NG,)), DMA((NG,)), DMA, DMA((ND,)), DMA, DMA,
-                DMA((2,)), DMA((2, 3)), DMA((2, nch + 1)), DMA((2, nch + 1)),
+                DMA((2,)), DMA((2, 8)), DMA((2, 3)), DMA((2, nch + 2)), DMA((2, nch + 2)),
                 DMA((2, nch)), DMA((2, nch)), DMA((2, nch)),
                 DMA((2,)), DMA((2,)), DMA((2,)), DMA((2,)), DMA((2,)), DMA((2, 2, 2)),
             ],
@@ -450,10 +532,23 @@
                 collective_id=0, has_side_effects=True, vmem_limit_bytes=67_000_000),
             name="decode_step",
         )(hidden, norm_gain, w_q, w_kv, w_gate, w_up, w_o, w_down, k_cache, v_cache, seq_len)
-        slot_hit = (jnp.arange(cache_len)[None, :] == seq_len[:, None])[None, :, :, None]
-        k_out = jnp.where(slot_hit, k_new[:, :, None, :], k_cache)
-        v_out = jnp.where(slot_hit, v_new[:, :, None, :], v_cache)
-        return h_new, k_out, v_out
+        k_out, v_out, h_out = pl.pallas_call(
+            place_kernel,
+            out_shape=(
+                jax.ShapeDtypeStruct(k_cache.shape, BF),
+                jax.ShapeDtypeStruct(v_cache.shape, BF),
+                jax.ShapeDtypeStruct(hidden.shape, BF),
+            ),
+            in_specs=[anyspec] * 5 + [pl.BlockSpec(memory_space=pltpu.SMEM)],
+            out_specs=(anyspec,) * 3,
+            scratch_shapes=[
+                V((2, L, ns, hd), BF), V((rows, half), BF), V((2, L, ns, cache_len, hd), BF),
+                DMA((2,)), DMA, DMA((2, L)), DMA((2, L)),
+            ],
+            compiler_params=pltpu.CompilerParams(vmem_limit_bytes=60_000_000),
+            name="place_rows",
+        )(k_new, v_new, h_new, k_cache, v_cache, seq_len)
+        return h_out, k_out, v_out
 
     return jax.shard_map(
         device_step,

time: 118 us -> 112 us (0.949)
  other arithmetic: 5.67 us -> 0 us
    pallas_call x0 -> x1, Pallas kernels: none -> 5.8 us  [device_step(): pl.pallas_call(place_kernel, out_shape=(jax.ShapeDtypeStruct(k_cache.shap...]
    pallas_call x1, Pallas kernels: 111 us -> 105 us  [device_step(): pl.pallas_call(functools.partial(step_kernel, dims), out_shape=(jax.Shape...]
    select_n x1 -> x0, other arithmetic: 4.94 us -> none  [device_step(): v_out = jnp.where(slot_hit, v_new[:, :, None, :], v_cache)]
where the time goes in v3:
time: 112 us
  Pallas kernels  111 us (99%)
    pallas_call x1, Pallas kernels, device_step(): pl.pallas_call(functools.partial(step_kernel, dims), out_shape=(jax.Shape...  105 us
    pallas_call x1, Pallas kernels, device_step(): pl.pallas_call(place_kernel, out_shape=(jax.ShapeDtypeStruct(k_cache.shap...  5.8 us

profile of v3, /device:TPU:0, one launch (start us, length us, event | category | flops | bytes accessed | tf_op | source)
XLA Modules:
  0.0 111.9 jit_solution(10985003156908692465)
XLA Ops:
  0.6 105.5 %decode_step.1 = (bf16[64,512]{1,0:T(8,128)(2,1)}, bf16[3,8,256]{2,1,0:T(8,128)(2,1)}, bf16[3,8,256]{2,1,0:T(8,128)(2,1)}) custom-call(bf16[64,512]{1,0:T(8,128)(2,1)} %hid.1, bf16[3,1024]{1,0:T(4,128)(2,1)} %gain.1, bf16[3,1024,2048]{2,1,0:T(8,128)(2,1)} %wq.1, bf16[3,1024,256]{2,1,0:T(8,128)(2,1)} %wkv.1, bf16[3,1024,8192]{2,1,0:T(8,128)(2,1)} %wg.1, ...), custom_call_target="tpu_custom_call" | custom-call | tf_op jit(solution)/shard_map/decode_step/pallas_call | solution.py:504
  106.1 5.8 %place_rows.1 = (bf16[3,8,256,256]{3,2,1,0:T(8,128)(2,1)}, bf16[3,8,256,256]{3,2,1,0:T(8,128)(2,1)}, bf16[64,512]{1,0:T(8,128)(2,1)}) custom-call(bf16[3,8,256]{2,1,0:T(8,128)(2,1)} %get-tuple-element.9.kn, bf16[3,8,256]{2,1,0:T(8,128)(2,1)} %get-tuple-element.10.vn, bf16[64,512]{1,0:T(8,128)(2,1)} %get-tuple-element.11.hn, bf16[3,8,256,256]{3,2,1,0:T(8,128)(2,1)} %kc.3, ...), custom_call_target="tpu_custom_call" | custom-call | tf_op jit(solution)/shard_map/place_rows/pallas_call | solution.py:535

commit v4 on v3

--- a/solution.py
+++ b/solution.py
@@ -8,6 +8,7 @@
 from jax.sharding import PartitionSpec as P
 
 NORM_EPS = 1e-6
+SHRINK = 2.0 ** -64
 MESH = pl.DeviceIdType.MESH
 BF = jnp.bfloat16
 F32 = jnp.float32
@@ -20,14 +21,14 @@
 T_D = (10, 12, 15, 16, 17, 18, 19)
 T_EN = (8, 9, 10, 11, 12, 13, 14)
 T_EF = (12, 14, 17, 18, 19, 20, 21)
-T_QB, T_QC, T_ATT, T_OS, T_ON, T_OF, T_OE, T_LN = 0, 2, 5, 8, 10, 14, 16, 15
+T_QB, T_QC, T_ATT, T_OS, T_ON, T_OF, T_OE, T_LN = 0, 3, 6, 9, 11, 14, 16, 15
 STEPS = 22
 
 
 def step_kernel(dims, hid, gain, wq, wkv, wg, wu, wo, wd, kc, vc, lens,
                 hout, knew, vnew,
                 wq_b, wkv_b, wg_b, wu_b, wo_b, wd_b, k_b, v_b,
-                hin, h_b, u_b, acc, ss_s, ss_r, ss0, tot,
+                hin, h_b, u_b, acc, ss_s, ss_r, ss0, tot, sc_b,
                 part, rb, ib, m_all, part_q, rb_q, ib_q, zq, yq, ob, o_all, yx_s, yx_r,
                 sem_wq, sem_wkv, sem_g, sem_u, sem_wo, sem_d, sem_k, sem_v,
                 sem_h, sem_s0, sem_ss, sem_rb, sem_ib, sem_mp, sem_mq, sem_mf,
@@ -132,26 +133,39 @@
             total = total + ss0[k]
         tot[...] = total
 
-    def norm_exchange():
+    def sums(k, dev):
+        return rc(ss_s, ss_r.at[k], sp(sem_ss, k), dev)
+
+    def send_sums():
         ss_s[...] = row_sums(h_b[...].astype(F32))
-        cps = [rc(ss_s, ss_r.at[k], sp(sem_ss, k), dev)
-               for k, dev in enumerate((dev_p, dev_q, dev_d))]
-        for cpy in cps:
-            cpy.start()
-        for cpy in cps:
-            cpy.wait()
+        for k, dev in enumerate((dev_p, dev_q, dev_d)):
+            sums(k, dev).start()
+
+    def get_sums():
+        for k, dev in enumerate((dev_p, dev_q, dev_d)):
+            sums(k, dev).wait()
         tot[...] = (ss_s[...] + ss_r[0]) + (ss_r[1] + ss_r[2])
 
     @jax.named_scope("norm")
     def norm(l):
-        pl.when(l > 0)(norm_exchange)
+        pl.when(l > 0)(send_sums)
         gall = gain[...].astype(F32)
         g = gall[0:1]
         for k in range(1, L):
             g = jnp.where(l == k, gall[k:k + 1], g)
+        u_b[...] = (h_b[...].astype(F32) * (g * SHRINK)).astype(BF)
+
+    @jax.named_scope("scale")
+    def row_scale(l):
+        pl.when(l > 0)(get_sums)
         tot_col = jnp.sum(jnp.where(eye, jnp.broadcast_to(tot[0:1], eye.shape), 0.0), axis=1, keepdims=True)
-        inv = lax.rsqrt(tot_col / D + NORM_EPS)
-        u_b[...] = (h_b[...].astype(F32) * inv * g).astype(BF)
+        sc = jnp.broadcast_to(lax.rsqrt(tot_col / D + NORM_EPS) / SHRINK, eye.shape)
+        for r in range(4):
+            sc_b[r // 2, r % 2] = sc[16 * r:16 * r + 16]
+
+    def scaled(z):
+        sc = sc_b[cx, c][:, 0:1]
+        return jnp.where(sc > 0.0, z * sc, 0.0)
 
     def put_rows(dst, cols, val):
         v = val.astype(BF)
@@ -192,10 +206,11 @@
         to_q_q(k).start()
 
     @jax.named_scope("c_q")
-    def c_q():
+    def c_q(l):
+        row_scale(l)
         for k in range(2):
             to_q_q(k).wait()
-        z = (part_q[cx, c].astype(F32) + rb_q[cx].astype(F32)) + ib_q[...].astype(F32)
+        z = scaled((part_q[cx, c].astype(F32) + rb_q[cx].astype(F32)) + ib_q[...].astype(F32))
         zq[0] = z[0:8].astype(BF)
         zq[1] = z[8:16].astype(BF)
         rc(zq.at[1 - y], yq.at[y], sp(sem_zq), dev_y).start()
@@ -310,7 +325,7 @@
     def stage_c(j):
         rc(part.at[j, 1 - cx, c], ib.at[j], sp(sem_ib, j), dev_q).wait()
         z = (part[j, cx, c].astype(F32) + rb[j, cx].astype(F32)) + ib[j].astype(F32)
-        z = z.astype(BF).astype(F32)
+        z = scaled(z).astype(BF).astype(F32)
         gate, up = z[:, :CH], z[:, CH:]
         m_all[j, cx, c] = (jax.nn.silu(gate) * up).astype(BF)
         rc(m_all.at[j, cx, c], m_all.at[j, cx, c], sp(sem_mq, j), dev_q).start()
@@ -372,7 +387,7 @@
             pl.when((l == 0) & (t == 3))(lambda: start(cp_o(0)))
             at(T_QB, lambda: b_q(1))
             at(T_B, stage_b)
-            at(T_QC, c_q)
+            at(T_QC, lambda: c_q(l))
             at(T_OS, o_send)
             at(T_LN, lambda: last_near(l))
             at(T_D, stage_d)
@@ -516,7 +531,7 @@
                 V((q_cols, d_out), BF), V((ND, ch, d_out), BF),
                 V((ns, cache_len, hd), BF), V((ns, cache_len, hd), BF),
                 V((2, rows, half), BF), V((rows, d_out), BF), V((rows, d_out), BF), V((2, rows // 2, d_out), F32),
-                V((8, 128), F32), V((3, 8, 128), F32), V((8, 8, 128), F32), V((8, 128), F32),
+                V((8, 128), F32), V((3, 8, 128), F32), V((8, 8, 128), F32), V((8, 128), F32), V((2, 2, 16, 128), F32),
                 V((nch, 2, 2, 16, 2 * ch), BF), V((nch, 2, 16, 2 * ch), BF), V((nch, 16, 2 * ch), BF),
                 V((nch, 2, 2, 16, ch), BF),
                 V((2, 2, 16, zc), BF), V((2, 16, zc), BF), V((16, zc), BF),

time: 112 us -> 106 us (0.946)
  Pallas kernels: 111 us -> 106 us
    pallas_call x1, Pallas kernels: 105 us -> 99.7 us  [device_step(): pl.pallas_call(functools.partial(step_kernel, dims), out_shape=(jax.Shape...]
where the time goes in v4:
time: 106 us
  Pallas kernels  106 us (100%)
    pallas_call x1, Pallas kernels, device_step(): pl.pallas_call(functools.partial(step_kernel, dims), out_shape=(jax.Shape...  99.7 us
    pallas_call x1, Pallas kernels, device_step(): pl.pallas_call(place_kernel, out_shape=(jax.ShapeDtypeStruct(k_cache.shap...  5.8 us

profile of v4, /device:TPU:0, one launch (start us, length us, event | category | flops | bytes accessed | tf_op | source)
XLA Modules:
  0.0 106.2 jit_solution(2905095088591560196)
XLA Ops:
  0.6 99.7 %decode_step.1 = (bf16[64,512]{1,0:T(8,128)(2,1)}, bf16[3,8,256]{2,1,0:T(8,128)(2,1)}, bf16[3,8,256]{2,1,0:T(8,128)(2,1)}) custom-call(bf16[64,512]{1,0:T(8,128)(2,1)} %hid.1, bf16[3,1024]{1,0:T(4,128)(2,1)} %gain.1, bf16[3,1024,2048]{2,1,0:T(8,128)(2,1)} %wq.1, bf16[3,1024,256]{2,1,0:T(8,128)(2,1)} %wkv.1, bf16[3,1024,8192]{2,1,0:T(8,128)(2,1)} %wg.1, ...), custom_call_target="tpu_custom_call" | custom-call | tf_op jit(solution)/shard_map/decode_step/pallas_call | solution.py:519
  100.4 5.8 %place_rows.1 = (bf16[3,8,256,256]{3,2,1,0:T(8,128)(2,1)}, bf16[3,8,256,256]{3,2,1,0:T(8,128)(2,1)}, bf16[64,512]{1,0:T(8,128)(2,1)}) custom-call(bf16[3,8,256]{2,1,0:T(8,128)(2,1)} %get-tuple-element.9.kn, bf16[3,8,256]{2,1,0:T(8,128)(2,1)} %get-tuple-element.10.vn, bf16[64,512]{1,0:T(8,128)(2,1)} %get-tuple-element.11.hn, bf16[3,8,256,256]{3,2,1,0:T(8,128)(2,1)} %kc.3, ...), custom_call_target="tpu_custom_call" | custom-call | tf_op jit(solution)/shard_map/place_rows/pallas_call | solution.py:550

commit v5 on v4

--- a/solution.py
+++ b/solution.py
@@ -16,13 +16,19 @@
 CH = 1024
 NG = 7
 ND = 8
-T_B = (1, 2, 3, 4, 5, 6, 7, 8)
-T_C = (4, 6, 8, 9, 10, 11, 12, 14)
-T_D = (10, 12, 15, 16, 17, 18, 19)
-T_EN = (8, 9, 10, 11, 12, 13, 14)
-T_EF = (12, 14, 17, 18, 19, 20, 21)
-T_QB, T_QC, T_ATT, T_OS, T_ON, T_OF, T_OE, T_LN = 0, 3, 6, 9, 11, 14, 16, 15
-STEPS = 22
+NE = 3
+NF = 4
+T_A = (0, 1, 5, 6, 7)
+T_AL = (2, 3, 4)
+T_B = (1, 2, 6, 7, 8)
+C1, C2, C3 = 0, 5, 6
+T_C1, T_C2, T_C3 = (4, 5, 6, 7, 8), (10,), (11, 13)
+T_D = (9, 10, 11, 13, 14, 15, 16)
+T_EA = (10, 11, 12, 14)
+T_EN = (10, 12, 13)
+T_EF = (16, 17, 18)
+T_SC, T_QB, T_QC, T_ATT, T_OS, T_OF, T_OE, T_LN = 4, 0, 4, 7, 10, 14, 15, 15
+STEPS = 19
 
 
 def step_kernel(dims, hid, gain, wq, wkv, wg, wu, wo, wd, kc, vc, lens,
@@ -120,8 +126,9 @@
         hin[y] = hid[...]
         rc(hid, hin.at[1 - y], sp(sem_h), dev_y).wait_recv()
         half = hid.shape[1]
-        h_b[:, :half] = hin[0]
-        h_b[:, half:] = hin[1]
+        for g in range(2):
+            for n in range(2):
+                h_b[g, :, n * half:(n + 1) * half] = hin[n, g * (rows // 2):(g + 1) * (rows // 2)]
         h_send.wait_send()
         for cpy in s0:
             cpy.wait_send()
@@ -137,7 +144,7 @@
         return rc(ss_s, ss_r.at[k], sp(sem_ss, k), dev)
 
     def send_sums():
-        ss_s[...] = row_sums(h_b[...].astype(F32))
+        ss_s[...] = row_sums(h_b[...].reshape(rows, 2 * half).astype(F32))
         for k, dev in enumerate((dev_p, dev_q, dev_d)):
             sums(k, dev).start()
 
@@ -146,14 +153,12 @@
             sums(k, dev).wait()
         tot[...] = (ss_s[...] + ss_r[0]) + (ss_r[1] + ss_r[2])
 
-    @jax.named_scope("norm")
-    def norm(l):
-        pl.when(l > 0)(send_sums)
+    def make_u(l, g):
         gall = gain[...].astype(F32)
-        g = gall[0:1]
+        gl = gall[0:1]
         for k in range(1, L):
-            g = jnp.where(l == k, gall[k:k + 1], g)
-        u_b[...] = (h_b[...].astype(F32) * (g * SHRINK)).astype(BF)
+            gl = jnp.where(l == k, gall[k:k + 1], gl)
+        u_b[g] = (h_b[g].astype(F32) * (gl * SHRINK)).astype(BF)
 
     @jax.named_scope("scale")
     def row_scale(l):
@@ -163,8 +168,8 @@
         for r in range(4):
             sc_b[r // 2, r % 2] = sc[16 * r:16 * r + 16]
 
-    def scaled(z):
-        sc = sc_b[cx, c][:, 0:1]
+    def scaled(z, g):
+        sc = sc_b[g, c][:, 0:1]
         return jnp.where(sc > 0.0, z * sc, 0.0)
 
     def put_rows(dst, cols, val):
@@ -185,7 +190,7 @@
     @jax.named_scope("a_q")
     def a_q(l):
         wait(cp_q(l))
-        u = u_b[...]
+        u = u_b[...].reshape(rows, u_b.shape[2])
         for k in range(2):
             for n in range(k * QC // 2, (k + 1) * QC // 2, 512):
                 put_rows(part_q, slice(n, n + 512), jnp.dot(u, wq_b[:, n:n + 512], preferred_element_type=F32))
@@ -207,10 +212,9 @@
 
     @jax.named_scope("c_q")
     def c_q(l):
-        row_scale(l)
         for k in range(2):
             to_q_q(k).wait()
-        z = scaled((part_q[cx, c].astype(F32) + rb_q[cx].astype(F32)) + ib_q[...].astype(F32))
+        z = scaled((part_q[cx, c].astype(F32) + rb_q[cx].astype(F32)) + ib_q[...].astype(F32), cx)
         zq[0] = z[0:8].astype(BF)
         zq[1] = z[8:16].astype(BF)
         rc(zq.at[1 - y], yq.at[y], sp(sem_zq), dev_y).start()
@@ -276,134 +280,251 @@
         rc(o_all.at[1 - cx, c], o_all.at[1 - cx, c], sp(sem_oq), dev_q).wait_recv()
         rc(o_all.at[1 - cx, c], o_all.at[1 - cx, c], sp(sem_of), dev_p).start()
 
-    def o_rows(g):
-        blocks = [o_all[g, i // 2, i % 2].astype(F32) for i in range(4)]
-        lhs = jnp.concatenate(blocks, axis=0).astype(BF)
-        for n in range(0, acc.shape[2], 512):
-            acc[g, :, n:n + 512] += jnp.dot(lhs, wo_b[:, n:n + 512], preferred_element_type=F32)
-
-    @jax.named_scope("o_near")
-    def o_near(l):
+    @jax.named_scope("o_all_rows")
+    def o_out(l):
         rc(o_all.at[cx, c], o_all.at[cx, 1 - c], sp(sem_op), dev_p).wait()
-        wait(cp_o(l))
-        o_rows(cx)
-
-    @jax.named_scope("o_far")
-    def o_far(l):
         rc(o_all.at[1 - cx, c], o_all.at[1 - cx, 1 - c], sp(sem_of), dev_p).wait()
         rc(o_all.at[cx, c], o_all.at[cx, c], sp(sem_oq), dev_q).wait_send()
-        o_rows(1 - cx)
+        wait(cp_o(l))
+        blocks = [o_all[i // 4, (i // 2) % 2, i % 2].astype(F32) for i in range(8)]
+        lhs = jnp.concatenate(blocks, axis=0).astype(BF)
+        hr = rows // 2
+        for n in range(0, acc.shape[2], 512):
+            v = jnp.dot(lhs, wo_b[:, n:n + 512], preferred_element_type=F32)
+            for g in range(2):
+                acc[g, :, n:n + 512] += v[g * hr:(g + 1) * hr]
 
         @pl.when(l + 1 < L)
         def _():
             start(cp_o(l + 1))
+
+    def own(l):
+        return lax.rem(cx + l, 2)
+
+    def gu_products(l, j, u, put):
+        s = lax.rem(l * NCH + j, NG)
+        for n in range(0, CH, 512):
+            put(slice(n, n + 512), jnp.dot(u, wg_b[s, :, n:n + 512], preferred_element_type=F32))
+            put(slice(CH + n, CH + n + 512), jnp.dot(u, wu_b[s, :, n:n + 512], preferred_element_type=F32))
+
+    def half_rows(l, j, g):
+        def put(cols, val):
+            v = val.astype(BF)
+            for r in range(2):
+                part[j, g, r, :, cols] = v[16 * r:16 * r + 16]
+        gu_products(l, j, u_b[g], put)
+
+    def next_gu(i):
+        @pl.when(i + NG < L * NCH)
+        def _():
+            start(cp_gu(i + NG))
+
+    def to_p(j):
+        return rc(part.at[j, :, 1 - c], rb.at[j], sp(sem_rb, j), dev_p)
+
+    def to_p_half(j, g, k):
+        return rc(part.at[j, g, 1 - c], rb.at[j, g], sp(sem_rb, k), dev_p)
+
+    def to_q(l, j):
+        return rc(part.at[j, 1 - own(l), c], ib.at[j], sp(sem_ib, j), dev_q)
+
+    @jax.named_scope("a_early")
+    def a_early(l, j):
+        wait(cp_gu(l * NCH + j))
+        half_rows(l, j, 1 - own(l))
+        to_p_half(j, 1 - own(l), j).start()
+
+    @jax.named_scope("a_late")
+    def a_late(l, j):
+        half_rows(l, j, own(l))
+        to_p_half(j, own(l), NCH + 2 + j).start()
+        next_gu(l * NCH + j)
 
     @jax.named_scope("stage_a")
     def stage_a(l, j):
         i = l * NCH + j
-        s = lax.rem(i, NG)
         wait(cp_gu(i))
-        u = u_b[...]
         dst = part.at[j]
-        for n in range(0, CH, 512):
-            put_rows(dst, slice(n, n + 512), jnp.dot(u, wg_b[s, :, n:n + 512], preferred_element_type=F32))
-            put_rows(dst, slice(CH + n, CH + n + 512), jnp.dot(u, wu_b[s, :, n:n + 512], preferred_element_type=F32))
-        rc(part.at[j, :, 1 - c], rb.at[j], sp(sem_rb, j), dev_p).start()
-
-        @pl.when(i + NG < L * NCH)
-        def _():
-            start(cp_gu(i + NG))
+        gu_products(l, j, u_b[...].reshape(rows, u_b.shape[2]), lambda cols, val: put_rows(dst, cols, val))
+        to_p(j).start()
+        next_gu(i)
+
+    def add_to_q(l, j):
+        g = 1 - own(l)
+        s = part[j, g, c].astype(F32) + rb[j, g].astype(F32)
+        part[j, g, c] = s.astype(BF)
+        to_q(l, j).start()
+
+    @jax.named_scope("b_early")
+    def b_early(l, j):
+        to_p_half(j, 1 - own(l), j).wait()
+        add_to_q(l, j)
 
     @jax.named_scope("stage_b")
-    def stage_b(j):
-        rc(part.at[j, :, 1 - c], rb.at[j], sp(sem_rb, j), dev_p).wait()
-        s = part[j, 1 - cx, c].astype(F32) + rb[j, 1 - cx].astype(F32)
-        part[j, 1 - cx, c] = s.astype(BF)
-        rc(part.at[j, 1 - cx, c], ib.at[j], sp(sem_ib, j), dev_q).start()
+    def stage_b(l, j):
+        to_p(j).wait()
+        add_to_q(l, j)
 
     @jax.named_scope("stage_c")
-    def stage_c(j):
-        rc(part.at[j, 1 - cx, c], ib.at[j], sp(sem_ib, j), dev_q).wait()
-        z = (part[j, cx, c].astype(F32) + rb[j, cx].astype(F32)) + ib[j].astype(F32)
-        z = scaled(z).astype(BF).astype(F32)
+    def stage_c(l, j):
+        g = own(l)
+
+        @pl.when(j < NE)
+        def _():
+            to_p_half(j, g, NCH + 2 + j).wait()
+
+        to_q(l, j).wait()
+        z = (part[j, g, c].astype(F32) + rb[j, g].astype(F32)) + ib[j].astype(F32)
+        z = scaled(z, g).astype(BF).astype(F32)
         gate, up = z[:, :CH], z[:, CH:]
-        m_all[j, cx, c] = (jax.nn.silu(gate) * up).astype(BF)
-        rc(m_all.at[j, cx, c], m_all.at[j, cx, c], sp(sem_mq, j), dev_q).start()
+        m_all[j, g, c] = (jax.nn.silu(gate) * up).astype(BF)
+        m_send(j, g, sem_mq, dev_q).start()
 
         @pl.when(j == NCH - 1)
         def _():
-            rc(m_all.at[j, cx, c], m_all.at[j, cx, c], sp(sem_mf, j), dev_d).start()
-
-        rc(m_all.at[j, cx, c], m_all.at[j, cx, c], sp(sem_mp, j), dev_p).start()
+            m_send(j, g, sem_mf, dev_d).start()
+
+        m_send(j, g, sem_mp, dev_p).start()
+
+    def m_send(j, g, sem, dev):
+        return rc(m_all.at[j, g, c], m_all.at[j, g, c], sp(sem, j), dev)
+
+    def m_from(j, g, cc, sem, dev):
+        return rc(m_all.at[j, g, cc], m_all.at[j, g, cc], sp(sem, j), dev)
 
     @jax.named_scope("stage_d")
-    def stage_d(j):
-        rc(m_all.at[j, 1 - cx, c], m_all.at[j, 1 - cx, c], sp(sem_mq, j), dev_q).wait_recv()
-        rc(m_all.at[j, 1 - cx, c], m_all.at[j, 1 - cx, c], sp(sem_mf, j), dev_p).start()
+    def stage_d(l, j):
+        g = 1 - own(l)
+        m_from(j, g, c, sem_mq, dev_q).wait_recv()
+        m_send(j, g, sem_mf, dev_p).start()
 
     def e_rows(s, j, g):
         m = m_all[j, g].reshape(rows // 2, CH)
         for n in range(0, acc.shape[2], 512):
             acc[g, :, n:n + 512] += jnp.dot(m, wd_b[s, :, n:n + 512], preferred_element_type=F32)
 
+    def near_in(l, j):
+        m_send(j, own(l), sem_mp, dev_p).wait_send()
+        m_from(j, own(l), 1 - c, sem_mp, dev_p).wait_recv()
+        wait(cp_d(l * NCH + j))
+
+    def far_in(l, j):
+        g = 1 - own(l)
+        m_send(j, g, sem_mf, dev_p).wait_send()
+        m_from(j, g, 1 - c, sem_mf, dev_p).wait_recv()
+        m_send(j, own(l), sem_mq, dev_q).wait_send()
+
+    def next_d(i):
+        @pl.when(i + ND < L * NCH)
+        def _():
+            start(cp_d(i + ND))
+
+    @jax.named_scope("e_all")
+    def e_all(l, j):
+        i = l * NCH + j
+        near_in(l, j)
+        far_in(l, j)
+        s = lax.rem(i, ND)
+        m = m_all[j].reshape(rows, CH)
+        hr = rows // 2
+        for n in range(0, acc.shape[2], 512):
+            v = jnp.dot(m, wd_b[s, :, n:n + 512], preferred_element_type=F32)
+            for g in range(2):
+                acc[g, :, n:n + 512] += v[g * hr:(g + 1) * hr]
+        next_d(i)
+
     @jax.named_scope("e_near")
     def e_near(l, j):
-        i = l * NCH + j
-        rc(m_all.at[j, cx, c], m_all.at[j, cx, 1 - c], sp(sem_mp, j), dev_p).wait()
-        wait(cp_d(i))
-        e_rows(lax.rem(i, ND), j, cx)
+        near_in(l, j)
+        e_rows(lax.rem(l * NCH + j, ND), j, own(l))
 
     @jax.named_scope("e_far")
     def e_far(l, j):
         i = l * NCH + j
-        rc(m_all.at[j, 1 - cx, c], m_all.at[j, 1 - cx, 1 - c], sp(sem_mf, j), dev_p).wait()
-        rc(m_all.at[j, cx, c], m_all.at[j, cx, c], sp(sem_mq, j), dev_q).wait_send()
-        e_rows(lax.rem(i, ND), j, 1 - cx)
-
-        @pl.when(i + ND < L * NCH)
-        def _():
-            start(cp_d(i + ND))
+        far_in(l, j)
+        e_rows(lax.rem(i, ND), j, 1 - own(l))
+        next_d(i)
+
+    @jax.named_scope("take_rows")
+    def take_rows(g):
+        for n in range(2):
+            yx(g, n).wait_recv()
+        for n in range(2):
+            cols = slice(n * half, (n + 1) * half)
+            upd = yx_s[g, n].astype(F32) + yx_r[g, n].astype(F32)
+            h_b[g, :, cols] = (h_b[g, :, cols].astype(F32) + upd).astype(BF)
+
+    @jax.named_scope("last_sends")
+    def last_sends(l):
+        j = NCH - 1
+        m_send(j, own(l), sem_mq, dev_q).wait_send()
+        m_send(j, own(l), sem_mf, dev_d).wait_send()
+        for g in range(2):
+            yx(g, 1 - y).wait_send()
+            pl.when(l + 1 < L)(lambda: yx(g, y).wait_send())
 
     def layer(l, carry):
-        norm(l)
+        early = 1 - own(l)
+
+        @pl.when(l > 0)
+        def _():
+            take_rows(early)
+
+        make_u(l, early)
+        a_early(l, 0)
+        a_early(l, 1)
+        b_early(l, 0)
+        a_early(l, 2)
+        b_early(l, 1)
+
+        @pl.when(l > 0)
+        def _():
+            take_rows(1 - early)
+            send_sums()
+
+        make_u(l, 1 - early)
+        a_q(l)
         acc[...] = jnp.zeros_like(acc)
-        a_q(l)
-        b_q(0)
+        pl.when(l > 0)(lambda: last_sends(l - 1))
 
         def step(t, carry2):
-            def at(steps, fn):
+            def at(steps, fn, first=0):
                 if isinstance(steps, int):
                     pl.when(t == steps)(fn)
                     return
                 hit = t == steps[0]
-                j = jnp.int32(0)
+                j = jnp.int32(first)
                 for k, st in enumerate(steps[1:]):
                     hit = hit | (t == st)
-                    j = jnp.where(t >= st, k + 1, j)
+                    j = jnp.where(t >= st, first + k + 1, j)
                 pl.when(hit)(lambda: fn(j))
 
-            pl.when(t < NCH)(lambda: stage_a(l, t))
+            at(T_A, lambda j: stage_a(l, j), NE)
+            at(T_AL, lambda j: a_late(l, j))
             pl.when((l == 0) & (t < ND))(lambda: start(cp_d(t)))
             pl.when((l == 0) & (t == 3))(lambda: start(cp_o(0)))
+            at(T_QB, lambda: b_q(0))
             at(T_QB, lambda: b_q(1))
-            at(T_B, stage_b)
+            at(T_QB, lambda: b_early(l, 2))
+            at(T_B, lambda j: stage_b(l, j), NE)
+            at(T_SC, lambda: row_scale(l))
             at(T_QC, lambda: c_q(l))
+            at(T_D, lambda j: stage_d(l, j))
+            at(T_OE, lambda: o_out(l))
+            at(T_LN, lambda: last_near(l))
+            at(T_EA, lambda j: e_all(l, j))
             at(T_OS, o_send)
-            at(T_LN, lambda: last_near(l))
-            at(T_D, stage_d)
-            at(T_EN, lambda j: e_near(l, j))
-            at(T_ON, lambda: o_near(l))
-            at(T_OE, lambda: o_far(l))
-            at(T_EF, lambda j: e_far(l, j))
-            at(T_C, stage_c)
+            at(T_C1, lambda j: stage_c(l, j), C1)
+            at(T_C2, lambda j: stage_c(l, j), C2)
+            at(T_C3, lambda j: stage_c(l, j), C3)
+            at(T_EN, lambda j: e_near(l, j), NF)
+            at(T_EF, lambda j: e_far(l, j), NF)
             at(T_OF, o_fwd)
             at(T_ATT, lambda: attend(l))
             return carry2
 
         lax.fori_loop(0, STEPS, step, 0)
-
         last_far(l)
-        swap(l)
         return carry
 
     def yx(g, n):
@@ -423,46 +544,31 @@
     @jax.named_scope("last_near")
     def last_near(l):
         j = NCH - 1
-        i = l * NCH + j
-        rc(m_all.at[j, cx, c], m_all.at[j, cx, 1 - c], sp(sem_mp, j), dev_p).wait()
-        wait(cp_d(i))
-        last_rows(l, lax.rem(i, ND), cx)
+        near_in(l, j)
+        last_rows(l, lax.rem(l * NCH + j, ND), own(l))
 
     @jax.named_scope("last_far")
     def last_far(l):
         j = NCH - 1
         i = l * NCH + j
-        rc(m_all.at[j, cx, c], m_all.at[j, 1 - cx, c], sp(sem_mq, j), dev_q).wait_recv()
-        rc(m_all.at[j, cx, c], m_all.at[j, 1 - cx, 1 - c], sp(sem_mf, j), dev_d).wait_recv()
-        last_rows(l, lax.rem(i, ND), 1 - cx)
-
-        @pl.when(i + ND < L * NCH)
-        def _():
-            start(cp_d(i + ND))
+        g = 1 - own(l)
+        m_from(j, g, c, sem_mq, dev_q).wait_recv()
+        m_from(j, g, 1 - c, sem_mf, dev_d).wait_recv()
+        last_rows(l, lax.rem(i, ND), g)
+        next_d(i)
 
     @jax.named_scope("swap")
-    def swap(l):
-        rc(m_all.at[NCH - 1, cx, c], m_all.at[NCH - 1, cx, c], sp(sem_mq, NCH - 1), dev_q).wait_send()
-        rc(m_all.at[NCH - 1, cx, c], m_all.at[NCH - 1, cx, c], sp(sem_mf, NCH - 1), dev_d).wait_send()
-        for g in (cx, 1 - cx):
-            yx(g, y).wait_recv()
-            yx(g, 1 - y).wait_send()
-
-        @pl.when(l + 1 < L)
-        def _():
-            for g in (cx, 1 - cx):
-                yx(g, 1 - y).wait_recv()
-                yx(g, y).wait_send()
-
+    def finish():
         hr = rows // 2
         for g in range(2):
-            for n in range(2):
-                rr, cc = slice(g * hr, (g + 1) * hr), slice(n * half, (n + 1) * half)
-                upd = yx_s[g, n].astype(F32) + yx_r[g, n].astype(F32)
-                h_b[rr, cc] = (h_b[rr, cc].astype(F32) + upd).astype(BF)
+            yx(g, y).wait_recv()
+            cols = pl.ds(pl.multiple_of(y * half, half), half)
+            upd = yx_s[g, y].astype(F32) + yx_r[g, y].astype(F32)
+            hout[g * hr:(g + 1) * hr, :] = (h_b[g, :, cols].astype(F32) + upd).astype(BF)
+        last_sends(jnp.int32(L - 1))
 
     lax.fori_loop(0, L, layer, 0)
-    hout[...] = h_b[:, pl.ds(pl.multiple_of(y * half, half), half)]
+    finish()
 
 
 def place_kernel(kn, vn, hn, kc, vc, lens, ko, vo, ho, new_b, h_b, kv_b, sem_n, sem_h, sem_in, sem_out):
@@ -530,7 +636,7 @@
                 V((NG, k_in, ch), BF), V((NG, k_in, ch), BF),
                 V((q_cols, d_out), BF), V((ND, ch, d_out), BF),
                 V((ns, cache_len, hd), BF), V((ns, cache_len, hd), BF),
-                V((2, rows, half), BF), V((rows, d_out), BF), V((rows, d_out), BF), V((2, rows // 2, d_out), F32),
+                V((2, rows, half), BF), V((2, rows // 2, d_out), BF), V((2, rows // 2, d_out), BF), V((2, rows // 2, d_out), F32),
                 V((8, 128), F32), V((3, 8, 128), F32), V((8, 8, 128), F32), V((8, 128), F32), V((2, 2, 16, 128), F32),
                 V((nch, 2, 2, 16, 2 * ch), BF), V((nch, 2, 16, 2 * ch), BF), V((nch, 16, 2 * ch), BF),
                 V((nch, 2, 2, 16, ch), BF),
@@ -539,7 +645,7 @@
                 V((2, ns, q_cols), BF), V((2, 2, 2, ns, q_cols), BF),
                 V((2, 2, rows // 2, half), BF), V((2, 2, rows // 2, half), BF),
                 DMA, DMA, DMA((NG,)), DMA((NG,)), DMA, DMA((ND,)), DMA, DMA,
-                DMA((2,)), DMA((2, 8)), DMA((2, 3)), DMA((2, nch + 2)), DMA((2, nch + 2)),
+                DMA((2,)), DMA((2, 8)), DMA((2, 3)), DMA((2, nch + 2 + NE)), DMA((2, nch + 2)),
                 DMA((2, nch)), DMA((2, nch)), DMA((2, nch)),
                 DMA((2,)), DMA((2,)), DMA((2,)), DMA((2,)), DMA((2,)), DMA((2, 2, 2)),
             ],

time: 106 us -> 103 us (0.972)
  Pallas kernels: 106 us -> 102 us
    pallas_call x1, Pallas kernels: 99.7 us -> 96.4 us  [device_step(): pl.pallas_call(functools.partial(step_kernel, dims), out_shape=(jax.Shape...]
where the time goes in v5:
time: 103 us
  Pallas kernels  102 us (99%)
    pallas_call x1, Pallas kernels, device_step(): pl.pallas_call(functools.partial(step_kernel, dims), out_shape=(jax.Shape...  96.4 us
    pallas_call x1, Pallas kernels, device_step(): pl.pallas_call(place_kernel, out_shape=(jax.ShapeDtypeStruct(k_cache.shap...  5.8 us

profile of v5, /device:TPU:0, one launch (start us, length us, event | category | flops | bytes accessed | tf_op | source)
XLA Modules:
  0.0 102.9 jit_solution(8033009884255344898)
XLA Ops:
  0.6 96.4 %decode_step.1 = (bf16[64,512]{1,0:T(8,128)(2,1)}, bf16[3,8,256]{2,1,0:T(8,128)(2,1)}, bf16[3,8,256]{2,1,0:T(8,128)(2,1)}) custom-call(bf16[64,512]{1,0:T(8,128)(2,1)} %hid.1, bf16[3,1024]{1,0:T(4,128)(2,1)} %gain.1, bf16[3,1024,2048]{2,1,0:T(8,128)(2,1)} %wq.1, bf16[3,1024,256]{2,1,0:T(8,128)(2,1)} %wkv.1, bf16[3,1024,8192]{2,1,0:T(8,128)(2,1)} %wg.1, ...), custom_call_target="tpu_custom_call" | custom-call | tf_op jit(solution)/shard_map/decode_step/pallas_call | solution.py:625
  97.1 5.8 %place_rows.1 = (bf16[3,8,256,256]{3,2,1,0:T(8,128)(2,1)}, bf16[3,8,256,256]{3,2,1,0:T(8,128)(2,1)}, bf16[64,512]{1,0:T(8,128)(2,1)}) custom-call(bf16[3,8,256]{2,1,0:T(8,128)(2,1)} %get-tuple-element.9.kn, bf16[3,8,256]{2,1,0:T(8,128)(2,1)} %get-tuple-element.10.vn, bf16[64,512]{1,0:T(8,128)(2,1)} %get-tuple-element.11.hn, bf16[3,8,256,256]{3,2,1,0:T(8,128)(2,1)} %kc.3, ...), custom_call_target="tpu_custom_call" | custom-call | tf_op jit(solution)/shard_map/place_rows/pallas_call | solution.py:656

commit v6 on v5

--- a/solution.py
+++ b/solution.py
@@ -23,21 +23,22 @@
 T_B = (1, 2, 6, 7, 8)
 C1, C2, C3 = 0, 5, 6
 T_C1, T_C2, T_C3 = (4, 5, 6, 7, 8), (10,), (11, 13)
-T_D = (9, 10, 11, 13, 14, 15, 16)
+T_D = (9, 10, 11, 13, 14, 15)
 T_EA = (10, 11, 12, 14)
 T_EN = (10, 12, 13)
-T_EF = (16, 17, 18)
+T_EF = (15, 16, 17)
 T_SC, T_QB, T_QC, T_ATT, T_OS, T_OF, T_OE, T_LN = 4, 0, 4, 7, 10, 14, 15, 15
-STEPS = 19
+T_ON, T_LN0 = 13, 14
+STEPS = 18
 
 
 def step_kernel(dims, hid, gain, wq, wkv, wg, wu, wo, wd, kc, vc, lens,
                 hout, knew, vnew,
                 wq_b, wkv_b, wg_b, wu_b, wo_b, wd_b, k_b, v_b,
-                hin, h_b, u_b, acc, ss_s, ss_r, ss0, tot, sc_b,
+                hin, h_b, u_b, acc, ss_s, ss_r, tot, sc_b,
                 part, rb, ib, m_all, part_q, rb_q, ib_q, zq, yq, ob, o_all, yx_s, yx_r,
                 sem_wq, sem_wkv, sem_g, sem_u, sem_wo, sem_d, sem_k, sem_v,
-                sem_h, sem_s0, sem_ss, sem_rb, sem_ib, sem_mp, sem_mq, sem_mf,
+                sem_h, sem_ss, sem_rb, sem_ib, sem_mp, sem_mq, sem_mf,
                 sem_zq, sem_oy, sem_op, sem_oq, sem_of, sem_yx):
     L, NCH, D = dims["layers"], dims["n_chunks"], dims["d"]
     HD = 256
@@ -102,43 +103,32 @@
         row = jnp.sum(jnp.where(eye, ss, 0.0), axis=0, keepdims=True)
         return jnp.broadcast_to(row, tot.shape)
 
-    me = x * 2 + y
-    ss0[me] = row_sums(hid[...].astype(F32))
-
-    def other(k):
-        return {"x": lax.rem(x + k // 2, 4), "yz": lax.rem(y + k % 2, 2)}
-
     with jax.named_scope("barrier"):
         barrier = pltpu.get_barrier_semaphore()
-        for k in range(1, 8):
-            pl.semaphore_signal(barrier, inc=1, device_id=other(k), device_id_type=MESH)
-        pl.semaphore_wait(barrier, 7)
+        for dev in (dev_p, dev_q, dev_d, dev_y):
+            pl.semaphore_signal(barrier, inc=1, device_id=dev, device_id_type=MESH)
+        pl.semaphore_wait(barrier, 4)
 
     with jax.named_scope("hx"):
-        h_send = rc(hid, hin.at[y], sp(sem_h), dev_y)
-        h_send.start()
-        s0 = [rc(ss0.at[me], ss0.at[me], sp(sem_s0, k), other(k)) for k in range(1, 8)]
-        for cpy in s0:
-            cpy.start()
+        half = hid.shape[1]
+        hr = rows // 2
+
+        def h_rows(g, yy):
+            return rc(hid.at[pl.ds(pl.multiple_of(g * hr, hr), hr)], hin.at[yy, g], sp(sem_h, g), dev_y)
+
+        h_rows(1 - cx, y).start()
+        h_rows(cx, y).start()
         for k in range(4, NG):
             start(cp_gu(k))
         start(cp_kv(0))
-        hin[y] = hid[...]
-        rc(hid, hin.at[1 - y], sp(sem_h), dev_y).wait_recv()
-        half = hid.shape[1]
         for g in range(2):
-            for n in range(2):
-                h_b[g, :, n * half:(n + 1) * half] = hin[n, g * (rows // 2):(g + 1) * (rows // 2)]
-        h_send.wait_send()
-        for cpy in s0:
-            cpy.wait_send()
-        for k in range(1, 8):
-            frm = lax.rem(x + 4 - k // 2, 4) * 2 + lax.rem(y + 2 - k % 2, 2)
-            rc(ss0.at[frm], ss0.at[frm], sp(sem_s0, k), other(k)).wait_recv()
-        total = ss0[0]
-        for k in range(1, 8):
-            total = total + ss0[k]
-        tot[...] = total
+            hin[y, g] = hid[g * hr:(g + 1) * hr]
+
+    @jax.named_scope("first_rows")
+    def first_rows(g):
+        h_rows(g, 1 - y).wait_recv()
+        for n in range(2):
+            h_b[g, :, n * half:(n + 1) * half] = hin[n, g]
 
     def sums(k, dev):
         return rc(ss_s, ss_r.at[k], sp(sem_ss, k), dev)
@@ -162,7 +152,7 @@
 
     @jax.named_scope("scale")
     def row_scale(l):
-        pl.when(l > 0)(get_sums)
+        get_sums()
         tot_col = jnp.sum(jnp.where(eye, jnp.broadcast_to(tot[0:1], eye.shape), 0.0), axis=1, keepdims=True)
         sc = jnp.broadcast_to(lax.rsqrt(tot_col / D + NORM_EPS) / SHRINK, eye.shape)
         for r in range(4):
@@ -280,12 +270,39 @@
         rc(o_all.at[1 - cx, c], o_all.at[1 - cx, c], sp(sem_oq), dev_q).wait_recv()
         rc(o_all.at[1 - cx, c], o_all.at[1 - cx, c], sp(sem_of), dev_p).start()
 
+    def o_near_in(l):
+        rc(o_all.at[cx, c], o_all.at[cx, 1 - c], sp(sem_op), dev_p).wait()
+        wait(cp_o(l))
+
+    def o_far_in():
+        rc(o_all.at[1 - cx, c], o_all.at[1 - cx, 1 - c], sp(sem_of), dev_p).wait()
+        rc(o_all.at[cx, c], o_all.at[cx, c], sp(sem_oq), dev_q).wait_send()
+
+    def next_o(l):
+        @pl.when(l + 1 < L)
+        def _():
+            start(cp_o(l + 1))
+
+    def o_rows(g):
+        lhs = jnp.concatenate([o_all[g, i // 2, i % 2].astype(F32) for i in range(4)], axis=0).astype(BF)
+        for n in range(0, acc.shape[2], 512):
+            acc[g, :, n:n + 512] += jnp.dot(lhs, wo_b[:, n:n + 512], preferred_element_type=F32)
+
+    @jax.named_scope("o_near")
+    def o_near(l):
+        o_near_in(l)
+        o_rows(cx)
+
+    @jax.named_scope("o_far")
+    def o_far(l):
+        o_far_in()
+        o_rows(1 - cx)
+        next_o(l)
+
     @jax.named_scope("o_all_rows")
     def o_out(l):
-        rc(o_all.at[cx, c], o_all.at[cx, 1 - c], sp(sem_op), dev_p).wait()
-        rc(o_all.at[1 - cx, c], o_all.at[1 - cx, 1 - c], sp(sem_of), dev_p).wait()
-        rc(o_all.at[cx, c], o_all.at[cx, c], sp(sem_oq), dev_q).wait_send()
-        wait(cp_o(l))
+        o_near_in(l)
+        o_far_in()
         blocks = [o_all[i // 4, (i // 2) % 2, i % 2].astype(F32) for i in range(8)]
         lhs = jnp.concatenate(blocks, axis=0).astype(BF)
         hr = rows // 2
@@ -293,10 +310,7 @@
             v = jnp.dot(lhs, wo_b[:, n:n + 512], preferred_element_type=F32)
             for g in range(2):
                 acc[g, :, n:n + 512] += v[g * hr:(g + 1) * hr]
-
-        @pl.when(l + 1 < L)
-        def _():
-            start(cp_o(l + 1))
+        next_o(l)
 
     def own(l):
         return lax.rem(cx + l, 2)
@@ -466,10 +480,8 @@
     def layer(l, carry):
         early = 1 - own(l)
 
-        @pl.when(l > 0)
-        def _():
-            take_rows(early)
-
+        pl.when(l == 0)(lambda: first_rows(early))
+        pl.when(l > 0)(lambda: take_rows(early))
         make_u(l, early)
         a_early(l, 0)
         a_early(l, 1)
@@ -477,18 +489,21 @@
         a_early(l, 2)
         b_early(l, 1)
 
-        @pl.when(l > 0)
-        def _():
-            take_rows(1 - early)
-            send_sums()
-
+        pl.when(l == 0)(lambda: first_rows(1 - early))
+        pl.when(l > 0)(lambda: take_rows(1 - early))
+        send_sums()
         make_u(l, 1 - early)
         a_q(l)
         acc[...] = jnp.zeros_like(acc)
         pl.when(l > 0)(lambda: last_sends(l - 1))
 
+        @pl.when(l == 0)
+        def _():
+            for g in range(2):
+                h_rows(g, y).wait_send()
+
         def step(t, carry2):
-            def at(steps, fn, first=0):
+            def at(steps, fn, first=0, t=t):
                 if isinstance(steps, int):
                     pl.when(t == steps)(fn)
                     return
@@ -509,17 +524,21 @@
             at(T_B, lambda j: stage_b(l, j), NE)
             at(T_SC, lambda: row_scale(l))
             at(T_QC, lambda: c_q(l))
+            at(T_EF, lambda j: e_far(l, j), NF)
             at(T_D, lambda j: stage_d(l, j))
-            at(T_OE, lambda: o_out(l))
-            at(T_LN, lambda: last_near(l))
+            pl.when((t == T_ON) & (l == 0))(lambda: o_near(l))
+            pl.when((t == T_OE) & (l > 0))(lambda: o_out(l))
+            at(T_OE, lambda: stage_d(l, NCH - 2))
+            pl.when((t == T_LN) & (l > 0))(lambda: last_near(l))
             at(T_EA, lambda j: e_all(l, j))
             at(T_OS, o_send)
             at(T_C1, lambda j: stage_c(l, j), C1)
             at(T_C2, lambda j: stage_c(l, j), C2)
             at(T_C3, lambda j: stage_c(l, j), C3)
             at(T_EN, lambda j: e_near(l, j), NF)
-            at(T_EF, lambda j: e_far(l, j), NF)
             at(T_OF, o_fwd)
+            pl.when((t == T_LN0) & (l == 0))(lambda: last_near(l))
+            pl.when((t == T_OE) & (l == 0))(lambda: o_far(l))
             at(T_ATT, lambda: attend(l))
             return carry2
 
@@ -636,8 +655,8 @@
                 V((NG, k_in, ch), BF), V((NG, k_in, ch), BF),
                 V((q_cols, d_out), BF), V((ND, ch, d_out), BF),
                 V((ns, cache_len, hd), BF), V((ns, cache_len, hd), BF),
-                V((2, rows, half), BF), V((2, rows // 2, d_out), BF), V((2, rows // 2, d_out), BF), V((2, rows // 2, d_out), F32),
-                V((8, 128), F32), V((3, 8, 128), F32), V((8, 8, 128), F32), V((8, 128), F32), V((2, 2, 16, 128), F32),
+                V((2, 2, rows // 2, half), BF), V((2, rows // 2, d_out), BF), V((2, rows // 2, d_out), BF), V((2, rows // 2, d_out), F32),
+                V((8, 128), F32), V((3, 8, 128), F32), V((8, 128), F32), V((2, 2, 16, 128), F32),
                 V((nch, 2, 2, 16, 2 * ch), BF), V((nch, 2, 16, 2 * ch), BF), V((nch, 16, 2 * ch), BF),
                 V((nch, 2, 2, 16, ch), BF),
                 V((2, 2, 16, zc), BF), V((2, 16, zc), BF), V((16, zc), BF),
@@ -645,7 +664,7 @@
                 V((2, ns, q_cols), BF), V((2, 2, 2, ns, q_cols), BF),
                 V((2, 2, rows // 2, half), BF), V((2, 2, rows // 2, half), BF),
                 DMA, DMA, DMA((NG,)), DMA((NG,)), DMA, DMA((ND,)), DMA, DMA,
-                DMA((2,)), DMA((2, 8)), DMA((2, 3)), DMA((2, nch + 2 + NE)), DMA((2, nch + 2)),
+                DMA((2, 2)), DMA((2, 3)), DMA((2, nch + 2 + NE)), DMA((2, nch + 2)),
                 DMA((2, nch)), DMA((2, nch)), DMA((2, nch)),
                 DMA((2,)), DMA((2,)), DMA((2,)), DMA((2,)), DMA((2,)), DMA((2, 2, 2)),
             ],

time: 103 us -> 101 us (0.981)
    pallas_call x1, Pallas kernels: 96.4 us -> 94.7 us  [device_step(): pl.pallas_call(functools.partial(step_kernel, dims), out_shape=(jax.Shape...]
where the time goes in v6:
time: 101 us
  Pallas kernels  101 us (100%)
    pallas_call x1, Pallas kernels, device_step(): pl.pallas_call(functools.partial(step_kernel, dims), out_shape=(jax.Shape...  94.7 us
    pallas_call x1, Pallas kernels, device_step(): pl.pallas_call(place_kernel, out_shape=(jax.ShapeDtypeStruct(k_cache.shap...  5.8 us

profile of v6, /device:TPU:0, one launch (start us, length us, event | category | flops | bytes accessed | tf_op | source)
XLA Modules:
  0.0 101.2 jit_solution(12170083113424606302)
XLA Ops:
  0.6 94.7 %decode_step.1 = (bf16[64,512]{1,0:T(8,128)(2,1)}, bf16[3,8,256]{2,1,0:T(8,128)(2,1)}, bf16[3,8,256]{2,1,0:T(8,128)(2,1)}) custom-call(bf16[64,512]{1,0:T(8,128)(2,1)} %hid.1, bf16[3,1024]{1,0:T(4,128)(2,1)} %gain.1, bf16[3,1024,2048]{2,1,0:T(8,128)(2,1)} %wq.1, bf16[3,1024,256]{2,1,0:T(8,128)(2,1)} %wkv.1, bf16[3,1024,8192]{2,1,0:T(8,128)(2,1)} %wg.1, ...), custom_call_target="tpu_custom_call" | custom-call | tf_op jit(solution)/shard_map/decode_step/pallas_call | solution.py:644
  95.4 5.8 %place_rows.1 = (bf16[3,8,256,256]{3,2,1,0:T(8,128)(2,1)}, bf16[3,8,256,256]{3,2,1,0:T(8,128)(2,1)}, bf16[64,512]{1,0:T(8,128)(2,1)}) custom-call(bf16[3,8,256]{2,1,0:T(8,128)(2,1)} %get-tuple-element.9.kn, bf16[3,8,256]{2,1,0:T(8,128)(2,1)} %get-tuple-element.10.vn, bf16[64,512]{1,0:T(8,128)(2,1)} %get-tuple-element.11.hn, bf16[3,8,256,256]{3,2,1,0:T(8,128)(2,1)} %kc.3, ...), custom_call_target="tpu_custom_call" | custom-call | tf_op jit(solution)/shard_map/place_rows/pallas_call | solution.py:675

commit v7 on v6

--- a/solution.py
+++ b/solution.py
@@ -21,11 +21,11 @@
 T_A = (0, 1, 5, 6, 7)
 T_AL = (2, 3, 4)
 T_B = (1, 2, 6, 7, 8)
-C1, C2, C3 = 0, 5, 6
-T_C1, T_C2, T_C3 = (4, 5, 6, 7, 8), (10,), (11, 13)
+C1, C2, C3 = 0, 4, 5
+T_C1, T_C2, T_C3 = (4, 5, 6, 7), (10,), (10, 11, 13)
 T_D = (9, 10, 11, 13, 14, 15)
 T_EA = (10, 11, 12, 14)
-T_EN = (10, 12, 13)
+T_EN = (11, 12, 13)
 T_EF = (15, 16, 17)
 T_SC, T_QB, T_QC, T_ATT, T_OS, T_OF, T_OE, T_LN = 4, 0, 4, 7, 10, 14, 15, 15
 T_ON, T_LN0 = 13, 14

time: 101 us -> 102 us (level)
    pallas_call x1, Pallas kernels: 94.7 us -> 95.8 us  [device_step(): pl.pallas_call(functools.partial(step_kernel, dims), out_shape=(jax.Shape...]
where the time goes in v7:
time: 102 us
  Pallas kernels  102 us (100%)
    pallas_call x1, Pallas kernels, device_step(): pl.pallas_call(functools.partial(step_kernel, dims), out_shape=(jax.Shape...  95.8 us
    pallas_call x1, Pallas kernels, device_step(): pl.pallas_call(place_kernel, out_shape=(jax.ShapeDtypeStruct(k_cache.shap...  5.8 us

profile of v7, /device:TPU:0, one launch (start us, length us, event | category | flops | bytes accessed | tf_op | source)
XLA Modules:
  0.0 102.2 jit_solution(3999395656950604963)
XLA Ops:
  0.6 95.8 %decode_step.1 = (bf16[64,512]{1,0:T(8,128)(2,1)}, bf16[3,8,256]{2,1,0:T(8,128)(2,1)}, bf16[3,8,256]{2,1,0:T(8,128)(2,1)}) custom-call(bf16[64,512]{1,0:T(8,128)(2,1)} %hid.1, bf16[3,1024]{1,0:T(4,128)(2,1)} %gain.1, bf16[3,1024,2048]{2,1,0:T(8,128)(2,1)} %wq.1, bf16[3,1024,256]{2,1,0:T(8,128)(2,1)} %wkv.1, bf16[3,1024,8192]{2,1,0:T(8,128)(2,1)} %wg.1, ...), custom_call_target="tpu_custom_call" | custom-call | tf_op jit(solution)/shard_map/decode_step/pallas_call | solution.py:644
  96.4 5.8 %place_rows.1 = (bf16[3,8,256,256]{3,2,1,0:T(8,128)(2,1)}, bf16[3,8,256,256]{3,2,1,0:T(8,128)(2,1)}, bf16[64,512]{1,0:T(8,128)(2,1)}) custom-call(bf16[3,8,256]{2,1,0:T(8,128)(2,1)} %get-tuple-element.9.kn, bf16[3,8,256]{2,1,0:T(8,128)(2,1)} %get-tuple-element.10.vn, bf16[64,512]{1,0:T(8,128)(2,1)} %get-tuple-element.11.hn, bf16[3,8,256,256]{3,2,1,0:T(8,128)(2,1)} %kc.3, ...), custom_call_target="tpu_custom_call" | custom-call | tf_op jit(solution)/shard_map/place_rows/pallas_call | solution.py:675
